TPU v7x, 32 devices: a whole 2x2x4 slice. The times are simulated.
32 devices in a mesh: dp: 2 (over x), row: 4 (over z), col: 4 (over y, core).
Axes of the slice: x: 2, y: 2, z: 4, core: 2. Of those that a mesh axis runs over, the one named last changes fastest.
Arguments:
- x: bfloat16 [2, 32, 512, 2048], P(None, ('dp', 'row', 'col')), parts along dimension 1
- idx: int32 [2, 32, 512, 6], P(None, ('dp', 'row', 'col')), parts along dimension 1
- gates: float32 [2, 32, 512, 6], P(None, ('dp', 'row', 'col')), parts along dimension 1
- wq: bfloat16 [2048, 2048], replicated
- wk: bfloat16 [2048, 2048], replicated
- wv: bfloat16 [2048, 2048], replicated
- wo: bfloat16 [2048, 2048], replicated
- gattn: float32 [2048], replicated
- gmoe: float32 [2048], replicated
- w1: bfloat16 [64, 2048, 1408], P(('row', 'col'))
- w3: bfloat16 [64, 2048, 1408], P(('row', 'col'))
- w2: bfloat16 [64, 1408, 2048], P(('row', 'col'))
Outputs:
- output: bfloat16 [2, 32, 512, 2048], P(None, ('dp', 'row', 'col')), parts along dimension 1
There are 2 independent parts. A program takes and returns all parts, laid end to end along the dimension named above; an argument that names none is the same for every part.
All inputs are finite; a program needn't handle non-finite values.
Results may differ from a plain program's by a relative error of at most 0.00883776.
Values are sent between devices in bfloat16 or wider.
A program may use at most 1 GiB of HBM per device.

v0:
```python
import jax
import jax.numpy as jnp
from jax import lax
from jax.sharding import PartitionSpec as P

HEAD = 128


def rms(v, g):
    vf = v.astype(jnp.float32)
    return (vf * lax.rsqrt(jnp.mean(vf * vf, axis=-1, keepdims=True) + 1e-6) * g).astype(jnp.bfloat16)


def attention(x, wq, wk, wv, wo, g):
    ns, seq, d = x.shape
    nh = wq.shape[1] // HEAD
    xf = x.reshape(ns * seq, d)
    u = rms(xf, g)

    def proj(w):
        a = jnp.dot(u, w, preferred_element_type=jnp.float32).astype(jnp.bfloat16)
        return a.reshape(ns, seq, nh, HEAD)

    q, k, v = proj(wq), proj(wk), proj(wv)
    causal = jnp.arange(seq)[:, None] >= jnp.arange(seq)[None, :]
    s = jnp.einsum("bqhe,bkhe->bhqk", q, k, preferred_element_type=jnp.float32) * HEAD ** -0.5
    s = jnp.where(causal, s, -1e30)
    p = jax.nn.softmax(s, axis=-1).astype(jnp.bfloat16)
    o = jnp.einsum("bhqk,bkhe->bqhe", p, v, preferred_element_type=jnp.float32).astype(jnp.bfloat16)
    o = o.reshape(ns * seq, nh * HEAD)
    a = jnp.dot(o, wo, preferred_element_type=jnp.float32)
    return (xf.astype(jnp.float32) + a).astype(jnp.bfloat16)


def capacity(t, top, n_exp):
    return ((top * ((2 * t + n_exp - 1) // n_exp) + 7) // 8) * 8


def slots(idx, n_exp, cap):
    t = idx.shape[0]
    hit = idx[:, :, None] == jnp.arange(n_exp, dtype=idx.dtype)
    cnt = jnp.sum(hit, axis=1).astype(jnp.bfloat16)
    tri = (jnp.arange(t)[:, None] > jnp.arange(t)[None, :]).astype(jnp.bfloat16)
    before = jnp.dot(tri, cnt, preferred_element_type=jnp.float32)
    pos = jnp.sum(jnp.where(hit, before[:, None, :], 0.0), axis=-1).astype(jnp.int32)
    return idx * cap + pos


def route(row, n):
    return row[:, :, None] == jnp.arange(n, dtype=row.dtype)


def dispatch(hit, z):
    sel = jnp.any(hit, axis=1).astype(jnp.bfloat16)
    return jnp.einsum("tr,td->rd", sel, z, preferred_element_type=jnp.float32).astype(jnp.bfloat16)


def combine(hit, g, back):
    t = g.shape[0]
    parts = []
    rest = g
    for _ in range(3):
        piece = rest.astype(jnp.bfloat16)
        parts.append(piece)
        rest = rest - piece.astype(jnp.float32)
    pieces = jnp.stack(parts)
    w = jnp.sum(jnp.where(hit[None], pieces[..., None], jnp.zeros((), jnp.bfloat16)), axis=2)
    out = jnp.dot(w.reshape(3 * t, -1), back, preferred_element_type=jnp.float32).reshape(3, t, -1)
    return out[0] + out[1] + out[2]


def solution(mesh):
    ep_axes = ("row", "col")
    tok_axes = ("dp", "row", "col")
    ep = mesh.shape["row"] * mesh.shape["col"]

    def local(x, idx, gates, wq, wk, wv, wo, gattn, gmoe, w1, w3, w2):
        ns, seq, d = x.shape[1:]
        t = ns * seq
        top = idx.shape[-1]
        el = w1.shape[0]
        n_exp = el * ep
        cap = capacity(t, top, n_exp)
        ys = []
        for m in range(2):
            h = attention(x[m], wq, wk, wv, wo, gattn)
            z = rms(h, gmoe)
            slot = slots(idx[m].reshape(t, top), n_exp, cap)
            hit = route(slot, n_exp * cap)
            buf = dispatch(hit, z)
            recv = lax.all_to_all(buf.reshape(ep, el * cap, d), ep_axes, 0, 0, tiled=True)
            recv = recv.reshape(ep, el, cap, d)
            h1 = jnp.einsum("secd,edf->secf", recv, w1, preferred_element_type=jnp.float32)
            h3 = jnp.einsum("secd,edf->secf", recv, w3, preferred_element_type=jnp.float32)
            act = (jax.nn.silu(h1) * h3).astype(jnp.bfloat16)
            out = jnp.einsum("secf,efd->secd", act, w2, preferred_element_type=jnp.float32).astype(jnp.bfloat16)
            back = lax.all_to_all(out.reshape(ep, el * cap, d), ep_axes, 0, 0, tiled=True)
            back = back.reshape(n_exp * cap, d)
            acc = combine(hit, gates[m].reshape(t, top), back)
            y = (h.astype(jnp.float32) + acc).astype(jnp.bfloat16)
            ys.append(y.reshape(ns, seq, d))
        return jnp.stack(ys)

    tok_spec = P(None, tok_axes)
    exp_spec = P(ep_axes)
    return jax.shard_map(local, mesh=mesh,
                         in_specs=(tok_spec, tok_spec, tok_spec, P(), P(), P(), P(), P(), P(), exp_spec, exp_spec, exp_spec),
                         out_specs=tok_spec, check_vma=False)
```

profile of v0, /device:TPU:19, one launch (start us, length us, event | category | flops | bytes accessed | tf_op | source)
XLA Modules:
  0.0 2360.6 jit_solution(11561337057736947957)
XLA Ops:
  0.1 0.7 fusion.102
  0.8 0.6 copy-done.6
  1.5 0.3 fusion.86
  1.9 20.5 fusion.79
  22.4 0.9 fusion.52
  23.3 8.3 convolution_convert_fusion.4
  31.7 2.5 copy.75
  34.2 8.7 fusion.85
  42.9 8.3 fusion.84
  51.2 8.1 fusion.64
  59.3 17.4 fusion.103
  76.6 7.7 fusion.80
  84.4 8.6 fusion.48
  93.0 17.4 convolution_convert_fusion
  110.4 7.0 all-to-all-start.2
  117.4 8.6 convolution_convert_fusion.7
  126.0 2.5 copy.74
  128.6 0.3 fusion.87
  129.0 8.7 fusion.83
  137.7 8.3 fusion.82
  146.0 8.2 fusion.69
  154.2 17.8 fusion.104
  172.0 7.7 fusion.81
  179.7 9.4 fusion.44
  189.1 18.8 fusion.78
  207.9 17.6 convolution_convert_fusion.1
  225.6 433.6 %all-to-all-done.2 = bf16[16,384,2048]{2,1,0:T(8,128)(2,1)} async-done(((bf16[16,384,2048]{2,1,0:T(8,128)(2,1)}), bf16[16,384,2048]{2,1,0:T(8,128)(2,1)}, u32[]{:S(2)}, u32[]{:S(2)}) %all-to-all-start.2) | async-done | bytes 25165856 | tf_op jit(solution)/shard_map/all_to_all | solution.py:91
  659.2 5.6 all-to-all-start
  664.8 47.8 %fusion.22 = f32[4,16,96,1408]{3,2,1,0:T(8,128)} fusion(bf16[4,2048,1408]{2,1,0:T(8,128)(2,1)} %param.21, bf16[16,4,96,2048]{3,2,1,0:T(8,128)(2,1)} %bitcast.33), kind=kOutput, calls=%fused_computation.30 | convolution fusion | flops 35433480192 | bytes 82837504 | tf_op jit(solution)/shard_map/secd,edf->secf/dot_general | solution.py:93
  712.6 52.0 %fusion.2 = bf16[16,4,96,1408]{3,2,0,1:T(8,128)(2,1)} fusion(f32[4,16,96,1408]{3,2,1,0:T(8,128)} %fusion.22, bf16[4,2048,1408]{2,1,0:T(8,128)(2,1)} %param.22, bf16[16,4,96,2048]{3,2,1,0:T(8,128)(2,1)} %bitcast.33), kind=kOutput, calls=%fused_computation.7 | convolution fusion | flops 35485384704 | bytes 100139008 | tf_op jit(solution)/shard_map/secd,edf->secf/dot_general | solution.py:94
  764.6 48.2 %convert_bitcast_fusion = bf16[16,4,96,2048]{3,2,0,1:T(8,128)(2,1)} fusion(bf16[16,4,96,1408]{3,2,0,1:T(8,128)(2,1)} %fusion.2, bf16[4,1408,2048]{2,1,0:T(8,128)(2,1)} %param.23), kind=kOutput, calls=%fused_computation.20 | convolution fusion | flops 35446063104 | bytes 65536000 | tf_op jit(solution)/shard_map/secf,efd->secd/dot_general | solution.py:96
  812.8 21.1 copy.68
  833.9 373.1 %all-to-all-done = bf16[16,384,2048]{2,1,0:T(8,128)(2,1)} async-done(((bf16[16,384,2048]{2,1,0:T(8,128)(2,1)}), bf16[16,384,2048]{2,1,0:T(8,128)(2,1)}, u32[]{:S(2)}, u32[]{:S(2)}) %all-to-all-start) | async-done | bytes 25165856 | tf_op jit(solution)/shard_map/all_to_all | solution.py:91
  1207.0 5.6 all-to-all-start.3
  1212.7 47.8 %fusion.24 = f32[4,16,96,1408]{3,2,1,0:T(8,128)} fusion(bf16[4,2048,1408]{2,1,0:T(8,128)(2,1)} %param.21, bf16[16,4,96,2048]{3,2,1,0:T(8,128)(2,1)} %bitcast.10), kind=kOutput, calls=%fused_computation.32 | convolution fusion | flops 35433480192 | bytes 82837504 | tf_op jit(solution)/shard_map/secd,edf->secf/dot_general | solution.py:93
  1260.5 52.0 %fusion.6 = bf16[16,4,96,1408]{3,2,0,1:T(8,128)(2,1)} fusion(f32[4,16,96,1408]{3,2,1,0:T(8,128)} %fusion.24, bf16[4,2048,1408]{2,1,0:T(8,128)(2,1)} %param.22, bf16[16,4,96,2048]{3,2,1,0:T(8,128)(2,1)} %bitcast.10), kind=kOutput, calls=%fused_computation.14 | convolution fusion | flops 35485384704 | bytes 100139008 | tf_op jit(solution)/shard_map/secd,edf->secf/dot_general | solution.py:94
  1312.5 48.0 %convert_bitcast_fusion.1 = bf16[16,4,96,2048]{3,2,0,1:T(8,128)(2,1)} fusion(bf16[16,4,96,1408]{3,2,0,1:T(8,128)(2,1)} %fusion.6, bf16[4,1408,2048]{2,1,0:T(8,128)(2,1)} %param.23), kind=kOutput, calls=%fused_computation.21 | convolution fusion | flops 35446063104 | bytes 65536000 | tf_op jit(solution)/shard_map/secf,efd->secd/dot_general | solution.py:96
  1360.5 21.0 copy.59
  1381.5 372.7 %all-to-all-done.3 = bf16[16,384,2048]{2,1,0:T(8,128)(2,1)} async-done(((bf16[16,384,2048]{2,1,0:T(8,128)(2,1)}), bf16[16,384,2048]{2,1,0:T(8,128)(2,1)}, u32[]{:S(2)}, u32[]{:S(2)}) %all-to-all-start.3) | async-done | bytes 25165856 | tf_op jit(solution)/shard_map/all_to_all | solution.py:97
  1754.3 5.9 all-to-all-start.1
  1760.4 75.0 %select_reduce_fusion = bf16[3,512,6144]{2,1,0:T(8,128)(2,1)} fusion(pred[512,6,6144]{2,0,1:T(8,128)(4,1)} %get-tuple-element.18, bf16[3,512,6]{1,2,0:T(8,128)(2,1)S(1)} %copy.65), kind=kLoop, calls=%fused_computation.2 | loop fusion | flops 103809024 | bytes 37767168 | tf_op jit(solution)/shard_map/reduce_sum | solution.py:67
  1835.4 75.0 %select_reduce_fusion.1 = bf16[3,512,6144]{2,1,0:T(8,128)(2,1)} fusion(pred[512,6,6144]{2,0,1:T(8,128)(4,1)} %get-tuple-element.16, bf16[3,512,6]{1,2,0:T(8,128)(2,1)S(1)} %copy.56), kind=kLoop, calls=%fused_computation.3 | loop fusion | flops 103809024 | bytes 37767168 | tf_op jit(solution)/shard_map/reduce_sum | solution.py:67
  1910.4 48.6 %fusion.106 = f32[1536,2048]{1,0:T(8,128)} fusion(bf16[1536,6144]{1,0:T(8,128)(2,1)} %bitcast.184, bf16[6144,2048]{1,0:T(8,128)(2,1)} %bitcast.41), kind=kOutput, calls=%fused_computation.157 | convolution fusion | flops 38654705664 | bytes 56623104 | tf_op jit(solution)/shard_map/dot_general | solution.py:68
  1959.0 6.9 fusion.60
  1965.9 336.3 %all-to-all-done.1 = bf16[16,384,2048]{2,1,0:T(8,128)(2,1)} async-done(((bf16[16,384,2048]{2,1,0:T(8,128)(2,1)}), bf16[16,384,2048]{2,1,0:T(8,128)(2,1)}, u32[]{:S(2)}, u32[]{:S(2)}) %all-to-all-start.1) | async-done | bytes 25165856 | tf_op jit(solution)/shard_map/all_to_all | solution.py:97
  2302.3 48.8 %fusion.105 = f32[1536,2048]{1,0:T(8,128)} fusion(bf16[1536,6144]{1,0:T(8,128)(2,1)} %bitcast.183, bf16[6144,2048]{1,0:T(8,128)(2,1)} %bitcast.21), kind=kOutput, calls=%fused_computation.156 | convolution fusion | flops 38654705664 | bytes 56623104 | tf_op jit(solution)/shard_map/dot_general | solution.py:68
  2351.1 6.9 fusion.62
  2358.0 2.4 pad_maximum_fusion
  (37 shorter events, 0.7 us)
Async XLA Ops:
  0.8 0.6 copy-start.6
  1.9 20.5 copy-start
  1.9 21.4 copy-start.9
  34.2 8.7 copy-start.1
  84.3 8.7 copy-start.3
  84.3 8.7 copy-start.10
  93.0 17.4 copy-start.4
  110.4 548.8 %all-to-all-start.2 = ((bf16[16,384,2048]{2,1,0:T(8,128)(2,1)}), bf16[16,384,2048]{2,1,0:T(8,128)(2,1)}, u32[]{:S(2)}, u32[]{:S(2)}) async-start(bf16[16,384,2048]{2,1,0:T(8,128)(2,1)} %bitcast.181), calls=%async_computation.2 | async-start | bytes 50331648 | tf_op jit(solution)/shard_map/all_to_all | solution.py:91
  129.0 8.7 copy-start.2
  179.7 9.4 copy-start.7
  189.1 18.8 copy-start.5
  659.2 547.9 %all-to-all-start = ((bf16[16,384,2048]{2,1,0:T(8,128)(2,1)}), bf16[16,384,2048]{2,1,0:T(8,128)(2,1)}, u32[]{:S(2)}, u32[]{:S(2)}) async-start(bf16[16,384,2048]{2,1,0:T(8,128)(2,1)} %bitcast.182), calls=%async_computation | async-start | bytes 50331648 | tf_op jit(solution)/shard_map/all_to_all | solution.py:91
  1207.0 547.2 %all-to-all-start.3 = ((bf16[16,384,2048]{2,1,0:T(8,128)(2,1)}), bf16[16,384,2048]{2,1,0:T(8,128)(2,1)}, u32[]{:S(2)}, u32[]{:S(2)}) async-start(bf16[16,384,2048]{2,1,0:T(8,128)(2,1)} %bitcast.180), calls=%async_computation.3 | async-start | bytes 50331648 | tf_op jit(solution)/shard_map/all_to_all | solution.py:97
  1754.3 6.0 copy-start.8
  1754.3 548.0 %all-to-all-start.1 = ((bf16[16,384,2048]{2,1,0:T(8,128)(2,1)}), bf16[16,384,2048]{2,1,0:T(8,128)(2,1)}, u32[]{:S(2)}, u32[]{:S(2)}) async-start(bf16[16,384,2048]{2,1,0:T(8,128)(2,1)} %bitcast.179), calls=%async_computation.1 | async-start | bytes 50331648 | tf_op jit(solution)/shard_map/all_to_all | solution.py:97
where the time goes:
time: 2370 us; the launch traced here: 2360 us
  waiting for transfers between devices  1520 us (64%)
  matrix products  529 us (22%)
  other arithmetic  242 us (10%)
  local copies, waits for them, and re-layouts  48.5 us (2%)
  starting transfers between devices  24.2 us (1%)
    all_to_all x2, waiting for transfers between devices, local(): lax.all_to_all(buf.reshape(ep, el * cap, d), ep_axes, 0, 0, tiled=True)  807 us
    all_to_all x2, waiting for transfers between devices, local(): lax.all_to_all(out.reshape(ep, el * cap, d), ep_axes, 0, 0, tiled=True)  709 us
    reduce_sum x2, other arithmetic, combine(): jnp.sum(jnp.where(hit[None], pieces[..., None], jnp.zeros((), jnp.bfloat1...  150 us
    dot_general x2, matrix products, local(): jnp.einsum('secd,edf->secf', recv, w3, preferred_element_type=jnp.float32)  104 us
    dot_general x2, matrix products, combine(): jnp.dot(w.reshape(3 * t, -1), back, preferred_element_type=jnp.float32)  97.4 us
    dot_general x2, matrix products, local(): jnp.einsum('secf,efd->secd', act, w2, preferred_element_type=jnp.float32)  96.2 us
    dot_general x2, matrix products, local(): jnp.einsum('secd,edf->secf', recv, w1, preferred_element_type=jnp.float32)  95.6 us
    dot_general x6, matrix products, proj(): a = jnp.dot(u, w, preferred_element_type=jnp.float32).astype(jnp.bfloat16)  50.9 us
  transfers between devices with their start and end apart: 4, of which 4 were waited for; matrix products, arithmetic and copies ran while one was open for 28% of the time, Pallas kernels for 0%

commit v1 on v0

v1 whole, which is shorter than its diff:
```python
import functools

import jax
import jax.numpy as jnp
from jax import lax
from jax.experimental import pallas as pl
from jax.experimental.pallas import tpu as pltpu
from jax.sharding import PartitionSpec as P

HEAD = 128
LANES = 128
TILE = 128
WIDTH = 288
NONE = -(1 << 20)
F32, BF16, I32 = jnp.float32, jnp.bfloat16, jnp.int32
ANY = pl.BlockSpec(memory_space=pl.ANY)
SMEM = pl.BlockSpec(memory_space=pltpu.SMEM)
VMEM = pl.BlockSpec(memory_space=pltpu.VMEM)
MESH = pl.DeviceIdType.MESH
STEPS = ((0, 1, 3, 2), (2, 3, 1, 0))


def rms(v, g):
    vf = v.astype(F32)
    return (vf * lax.rsqrt(jnp.mean(vf * vf, axis=-1, keepdims=True) + 1e-6) * g).astype(BF16)


def attention(x, wq, wk, wv, wo, g):
    ns, seq, d = x.shape
    nh = wq.shape[1] // HEAD
    xf = x.reshape(ns * seq, d)
    u = rms(xf, g)

    def proj(w):
        a = jnp.dot(u, w, preferred_element_type=F32).astype(BF16)
        return a.reshape(ns, seq, nh, HEAD)

    q, k, v = proj(wq), proj(wk), proj(wv)
    causal = jnp.arange(seq)[:, None] >= jnp.arange(seq)[None, :]
    s = jnp.einsum("bqhe,bkhe->bhqk", q, k, preferred_element_type=F32) * HEAD ** -0.5
    s = jnp.where(causal, s, -1e30)
    p = jax.nn.softmax(s, axis=-1).astype(BF16)
    o = jnp.einsum("bhqk,bkhe->bqhe", p, v, preferred_element_type=F32).astype(BF16)
    a = jnp.dot(o.reshape(ns * seq, nh * HEAD), wo, preferred_element_type=F32)
    return (xf.astype(F32) + a).astype(BF16)


def capacity(t, top, n_exp):
    return ((top * ((2 * t + n_exp - 1) // n_exp) + 7) // 8) * 8


def split3(v):
    a = v.astype(BF16)
    r = v - a.astype(F32)
    b = r.astype(BF16)
    return a, b, (r - b.astype(F32)).astype(BF16)


def ranks(hit):
    t = hit.shape[-1]
    tri = (jnp.arange(t)[:, None] < jnp.arange(t)[None, :]).astype(BF16)
    n = jnp.dot(hit.reshape(-1, t).astype(BF16), tri, preferred_element_type=F32).astype(I32)
    return jnp.where(hit, n.reshape(hit.shape), NONE)


def among(idx, first, n):
    e = first + jnp.arange(n, dtype=I32)
    return idx[:, :, None, :] == e[None, None, :, None]


def layer_kernel(cap, steps, z, h, lists, homes, px, pb, gb, w1, w3, w2,
                 y, ls, za, zy, zk, eo, em, ei, po, pm, pi, sr, rr,
                 zin, zb, x, act, w13b, w2b, ob, lsem, wsem, send, recv, ksend, krecv):
    el, d, f = w1.shape
    nm, t, _ = z.shape
    nb = steps * nm
    width = zb.shape[1]
    rows = el * cap
    fb = f // LANES
    quarter = d // 4
    dp, row, col = lax.axis_index("dp"), lax.axis_index("row"), lax.axis_index("col")
    core = (dp, row, col + 1 - 2 * lax.rem(col, 2))
    chip = (dp, row, col + 2 - 4 * (col // 2))

    def other(r):
        return (dp, lax.rem(row + r + steps, steps), col)

    def step_of(n):
        i = lax.rem(n, steps)
        i = i + (n // steps) * (steps - 1 - 2 * i)
        return lax.rem(i * (i + 1) // 2, steps)

    def remote(src, dst, kind, n, device):
        return pltpu.make_async_remote_copy(src_ref=src.at[n], dst_ref=dst.at[n], send_sem=send.at[kind, n],
                                            recv_sem=recv.at[kind, n], device_id=device, device_id_type=MESH)

    def go_row(n):
        return remote(ls, za, 0, n, other(step_of(n)))

    def go_chip(n):
        return remote(za, zy, 1, n, chip)

    def go_core(n, i):
        return pltpu.make_async_remote_copy(src_ref=(zy, za)[i].at[n], dst_ref=zk.at[n, i], send_sem=ksend.at[n, i],
                                            recv_sem=krecv.at[n, i], device_id=core, device_id_type=MESH)

    def go_expert(n):
        return remote(eo, ei, 2, n, core)

    def go_part(n):
        return remote(po, pi, 3, n, chip)

    def go_sum(n):
        return remote(sr, rr, 4, n, other(-step_of(n)))

    def local(src, dst, k):
        return pltpu.make_async_copy(src, dst, lsem.at[k])

    def run(*copies):
        for c in copies:
            c.start()
        for c in copies:
            c.wait()

    def weights(e, s):
        cs = []
        for i in range(fb):
            for o, w in enumerate((w1, w3)):
                cs.append(pltpu.make_async_copy(w.at[e, :, pl.ds(i * LANES, LANES)],
                                                w13b.at[s, :, pl.ds((2 * i + o) * LANES, LANES)],
                                                wsem.at[s, 2 * i + o]))
        cs.append(pltpu.make_async_copy(w2.at[e], w2b.at[s], wsem.at[s, 2 * fb]))
        return cs

    def hot(at, n):
        return lax.broadcasted_iota(I32, (n, at.shape[-1]), 0) == at

    barrier = pltpu.get_barrier_semaphore()
    partners = [core, chip] + [other(r) for r in range(1, steps)]
    for p in partners:
        pl.semaphore_signal(barrier, inc=1, device_id=p, device_id_type=MESH)
    for e in range(2):
        for c in weights(e, e):
            c.start()
    pl.semaphore_wait(barrier, len(partners))

    for m in range(nm):
        run(local(z.at[m], zin, 0))
        for i, r in enumerate(STEPS[m]):
            n = m * steps + i
            put = local(zb.at[i % 2], (za if r == 0 else ls).at[n], 1 + i % 2)
            sel = jnp.where(hot(lists[m, r:r + 1, :], width), 1.0, 0.0).astype(BF16)
            for c in range(4):
                cols = slice(c * quarter, (c + 1) * quarter)
                zb[i % 2, :, cols] = jnp.dot(sel, zin[:, cols], preferred_element_type=F32).astype(BF16)
            run(put)
            if r:
                go_row(n).start()
            elif m == 0:
                go_chip(n).start()

    go_row(1).wait_recv()
    go_chip(1).start()
    go_chip(0).wait_recv()
    for i in range(2):
        go_core(0, i).start()

    def dispatch(n):
        @pl.when(n + 1 < nb)
        def _():
            go_chip(n + 1).wait_recv()
            for i in range(2):
                go_core(n + 1, i).start()

        @pl.when(n + 2 < nb)
        def _():
            @pl.when(step_of(n + 2) != 0)
            def _():
                go_row(n + 2).wait_recv()
            go_chip(n + 2).start()

    def experts(n):
        for i in range(2):
            go_core(n, i).wait_recv()
        srcs = (zk.at[n, 0], zk.at[n, 1], zy.at[n], za.at[n])
        fetch = lambda i: local(srcs[i], zb.at[i % 2], 1 + i % 2)
        fetch(0).start()
        for i in range(4):
            if i + 1 < 4:
                fetch(i + 1).start()
            fetch(i).wait()
            sel = jnp.concatenate([jnp.where(hot(px[n, i * el + e:i * el + e + 1, :], cap), 1.0, 0.0).astype(BF16)
                                   for e in range(el)], 0)
            for c in range(4):
                cols = slice(c * quarter, (c + 1) * quarter)
                v = jnp.dot(sel, zb[i % 2, :, cols], preferred_element_type=F32).astype(BF16)
                for e in range(el):
                    x[e * rows + i * cap:e * rows + (i + 1) * cap, cols] = v[e * cap:(e + 1) * cap]

        def put(e, i):
            return pltpu.make_async_copy(x.at[pl.ds(pl.multiple_of(e * rows + i * cap, 32), cap)],
                                         (eo if i < 2 else em).at[n, i % 2, pl.ds(pl.multiple_of(e * cap, 32), cap)],
                                         lsem.at[3 + i])

        def expert(e, carry):
            s = lax.rem(e, 2)
            for c in weights(e, s):
                c.wait()

            def tile(k, cc):
                at = pl.ds(pl.multiple_of(e * rows + k * TILE, TILE), TILE)
                for c in range(fb):
                    v = jnp.dot(x[at, :], w13b[s, :, 2 * c * LANES:2 * (c + 1) * LANES], preferred_element_type=F32)
                    act[:, c * LANES:(c + 1) * LANES] = (jax.nn.silu(v[:, :LANES]) * v[:, LANES:]).astype(BF16)
                for c in range(d // (2 * LANES)):
                    cols = slice(2 * c * LANES, 2 * (c + 1) * LANES)
                    x[at, cols] = jnp.dot(act[...], w2b[s, :, cols], preferred_element_type=F32).astype(BF16)
                return cc
            lax.fori_loop(0, rows // TILE, tile, 0)
            run(*[put(e, i) for i in range(4)])

            @pl.when(n * el + e + 2 < nb * el)
            def _():
                for c in weights(lax.rem(e + 2, el), s):
                    c.start()
            return carry
        lax.fori_loop(0, el, expert, 0)
        go_expert(n).start()

    def combine(n):
        go_expert(n).wait_recv()
        fetch = lambda i: (local(em.at[n, i], x.at[pl.ds(2 * i * rows, rows)], 1 + 2 * i),
                           local(ei.at[n, i], x.at[pl.ds((2 * i + 1) * rows, rows)], 2 + 2 * i))
        for i in range(2):
            for c in fetch(i):
                c.start()
        k = 2 * el
        for i in range(2):
            m = jnp.concatenate([jnp.where(hot(pb[n, i * k + e:i * k + e + 1, :], cap), gb[n, i * k + e:i * k + e + 1, :], 0.0)
                                 for e in range(k)], 0)
            parts = split3(m)
            for c in fetch(i):
                c.wait()
            for c in range(4):
                cols = slice(c * quarter, (c + 1) * quarter)
                b = x[2 * i * rows:2 * (i + 1) * rows, cols]
                a = [lax.dot_general(p, b, (((0,), (0,)), ((), ())), preferred_element_type=F32) for p in parts]
                ob[i, :, cols] = a[0] + a[1] + a[2]
            put = local(ob.at[i], (po, pm)[i].at[n], 5 + i)
            put.start()
            if i == 0:
                put.wait()
                go_part(n).start()
            else:
                put.wait()

    def forward(n):
        go_part(n).wait_recv()

        @pl.when(step_of(n) != 0)
        def _():
            run(local(pm.at[n], ob.at[0], 1), local(pi.at[n], ob.at[1], 2))
            ob[0] = ob[0] + ob[1]
            run(local(ob.at[0], sr.at[n], 1))
            go_sum(n).start()

    def finish(m):
        at = [m * steps + STEPS[m].index(r) for r in range(steps)]
        for r in range(1, steps):
            go_sum(at[r]).wait_recv()
        refs = [pm.at[at[0]], pi.at[at[0]]] + [rr.at[at[r]] for r in range(1, steps)]
        lane = lax.broadcasted_iota(I32, (t, width), 1)
        fill = local(h.at[m], zin, 0)
        fill.start()
        fill.wait()
        for c in range(4):
            cols = slice(c * quarter, (c + 1) * quarter)
            spot = lambda l: ob.at[l // 4, :, pl.ds(l % 4 * quarter, quarter)]
            run(*[local(a.at[:, pl.ds(c * quarter, quarter)], spot(l), 1 + l) for l, a in enumerate(refs)])
            v = zin[:, cols].astype(F32)
            for r in range(steps):
                one = jnp.where(lane == homes[m, :, r:r + 1], 1.0, 0.0).astype(BF16)
                if r == 0:
                    u = ob[0, :, 0:quarter] + ob[0, :, quarter:2 * quarter]
                else:
                    l = r + 1
                    u = ob[l // 4, :, l % 4 * quarter:(l % 4 + 1) * quarter]
                for p in split3(u):
                    v = v + jnp.dot(one, p, preferred_element_type=F32)
            zin[:, cols] = v.astype(BF16)
        run(local(zin, y.at[m], 0))

    def block(n, carry):
        @pl.when(n < nb)
        def _():
            dispatch(n)
            experts(n)

        @pl.when(jnp.logical_and(n >= 1, n <= nb))
        def _():
            combine(n - 1)

        @pl.when(jnp.logical_and(n >= 2, n <= nb + 1))
        def _():
            forward(n - 2)

        @pl.when(n == nb - 1)
        def _():
            finish(0)

        @pl.when(n == nb + 2)
        def _():
            finish(1)
        return carry
    lax.fori_loop(0, nb + 3, block, 0)

    def drain(n, carry):
        for c in (go_chip(n), go_core(n, 0), go_core(n, 1), go_expert(n), go_part(n)):
            c.wait_send()

        @pl.when(step_of(n) != 0)
        def _():
            go_row(n).wait_send()
            go_sum(n).wait_send()
        return carry
    lax.fori_loop(0, nb, drain, 0)


def solution(mesh):
    ep_axes = ("row", "col")
    tok_axes = ("dp", "row", "col")
    nrow, ncol = mesh.shape["row"], mesh.shape["col"]
    ep = nrow * ncol

    def local(x, idx, gates, wq, wk, wv, wo, gattn, gmoe, w1, w3, w2):
        nm, ns, seq, d = x.shape
        t = ns * seq
        top = idx.shape[-1]
        el, _, f = w1.shape
        n_exp = el * ep
        layer = n_exp // nrow
        cap = capacity(t, top, n_exp)
        row, col = lax.axis_index("row"), lax.axis_index("col")
        me = row * ncol + col
        chip, core = col // 2, col % 2

        pay = jnp.concatenate([idx.astype(F32), gates, jnp.zeros((nm, ns, seq, 16 - 2 * top), F32)], -1)
        pay = jnp.swapaxes(pay.reshape(nm, t, 16), 1, 2)
        every = lax.all_gather(pay, tok_axes)
        every = every.reshape((-1, ep) + every.shape[1:])

        def width_needed():
            rows_of = every[:, :, :, :top] // layer
            hit = jnp.any(rows_of[..., None] == jnp.arange(nrow, dtype=F32), axis=3)
            return jnp.max(jnp.sum(hit.astype(I32), axis=3))

        need = width_needed()
        mine = lax.dynamic_index_in_dim(every, lax.axis_index("dp"), 0, keepdims=False)

        def flip(a, axis, bit):
            return jnp.where(bit == 0, jnp.flip(a, axis), a)

        def relative(a):
            a = a.reshape((nrow, 2, 2) + a.shape[1:])
            a = jnp.flip(lax.dynamic_slice_in_dim(jnp.concatenate([a, a]), row + 1, nrow), 0)
            return flip(flip(jnp.swapaxes(a, 1, 2), 1, core), 2, chip)

        def lists_of(m):
            steps = lax.rem(row + jnp.arange(nrow, dtype=I32), nrow)
            return ranks(jnp.any(idx[m].reshape(1, t, top) // layer == steps[:, None, None], 2))

        def routes(m, width):
            ia = relative(mine[:, m, :top].astype(I32)).reshape(ep, top, t)
            ga = relative(mine[:, m, top:2 * top])[:, 1].reshape(ep // 2, top, t)
            own = lambda a: a.reshape((nrow, 2, 2) + a.shape[1:])[:, 1].reshape((ep // 2,) + a.shape[1:])
            k = 2 * el
            hits = among(ia, k * (me // 2), k)
            pos = ranks(jnp.any(hits, 1))
            g = jnp.sum(jnp.where(own(hits), ga[:, :, None, :], 0.0), 1)
            listed = ranks(jnp.any(ia // layer == row, 1))
            lists = (listed[:, :, None] == jnp.arange(width, dtype=I32)).astype(BF16)
            places = jnp.einsum("pet,ptc->pec", (jnp.maximum(pos, -1) + 1).astype(BF16), lists,
                                preferred_element_type=F32).astype(I32) - 1
            gs = jnp.einsum("pet,ptc->pec", jnp.concatenate(split3(g), 1), own(lists), preferred_element_type=F32)
            lgate = gs[:, :k] + gs[:, k:2 * k] + gs[:, 2 * k:]
            turn = lambda a: jnp.where(core == 0, a, jnp.roll(a, el, axis=1))
            places = turn(places)
            lpos = own(places).reshape(nrow, 2 * k, width)
            lgate = turn(lgate).reshape(nrow, 2 * k, width)
            return places[:, :el].reshape(nrow, 4 * el, width), lpos, lgate

        def layers(width, zs, hs):
            lists = jnp.stack([lists_of(m) for m in range(nm)])
            homes = jnp.pad(jnp.swapaxes(lists, 1, 2), ((0, 0), (0, 0), (0, LANES - nrow)))
            rt = [routes(m, width) for m in range(nm)]
            px, pb, gb = (jnp.concatenate([jnp.stack([rt[m][k][r] for r in STEPS[m]]) for m in range(nm)]) for k in range(3))
            nb = nm * nrow
            rows = el * cap
            wide = jax.ShapeDtypeStruct((nb, width, d), BF16)
            exact = jax.ShapeDtypeStruct((nb, width, d), F32)
            pair = jax.ShapeDtypeStruct((nb, 2, rows, d), BF16)
            y, *_ = pl.pallas_call(
                functools.partial(layer_kernel, cap, nrow),
                out_shape=[jax.ShapeDtypeStruct((nm, t, d), BF16), wide, wide, wide,
                           jax.ShapeDtypeStruct((nb, 2, width, d), BF16), pair, pair, pair] + [exact] * 5,
                in_specs=[ANY] * 2 + [VMEM] * 5 + [ANY] * 3, out_specs=[ANY] * 13,
                scratch_shapes=[
                    pltpu.VMEM((t, d), BF16),
                    pltpu.VMEM((2, width, d), BF16),
                    pltpu.VMEM((4 * rows, d), BF16),
                    pltpu.VMEM((TILE, f), BF16),
                    pltpu.VMEM((2, d, 2 * f), BF16),
                    pltpu.VMEM((2, f, d), BF16),
                    pltpu.VMEM((2, width, d), F32),
                    pltpu.SemaphoreType.DMA((8,)),
                    pltpu.SemaphoreType.DMA((2, 2 * (f // LANES) + 1)),
                    pltpu.SemaphoreType.DMA((5, nb)),
                    pltpu.SemaphoreType.DMA((5, nb)),
                    pltpu.SemaphoreType.DMA((nb, 2)),
                    pltpu.SemaphoreType.DMA((nb, 2)),
                ],
                compiler_params=pltpu.CompilerParams(vmem_limit_bytes=67043328, has_side_effects=True,
                                                     collective_id=0 if width < t else 1),
                name="layer",
            )(zs, hs, lists, homes, px, pb, gb, w1, w3, w2)
            return y.reshape(nm, ns, seq, d)

        hs = jnp.stack([attention(x[m], wq, wk, wv, wo, gattn) for m in range(nm)])
        zs = rms(hs, gmoe)
        return lax.cond(need <= WIDTH, functools.partial(layers, WIDTH), functools.partial(layers, t), zs, hs)

    tok_spec = P(None, tok_axes)
    exp_spec = P(ep_axes)
    return jax.shard_map(local, mesh=mesh,
                         in_specs=(tok_spec, tok_spec, tok_spec, P(), P(), P(), P(), P(), P(), exp_spec, exp_spec, exp_spec),
                         out_specs=tok_spec, check_vma=False)
```

time: 2370 us -> 1060 us (0.45)
  the two profiles are of different devices: /device:TPU:19 before, /device:TPU:0 now
where the time goes in v1:
time: 1060 us; the launch traced here: 1050 us
  Pallas kernels  851 us (80%)
  matrix products  88.2 us (8%)
  other arithmetic  63.6 us (6%)
  local copies, waits for them, and re-layouts  28.8 us (3%)
  between operations  14.7 us (1%)
    pallas_call x1, Pallas kernels, layers(): pl.pallas_call(functools.partial(layer_kernel, cap, nrow), out_shape=[jax...  851 us
    sub x2, other arithmetic, attention(): p = jax.nn.softmax(s, axis=-1).astype(BF16)  45.2 us
    dot_general x6, matrix products, proj(): a = jnp.dot(u, w, preferred_element_type=F32).astype(BF16)  38 us
  transfers between devices with their start and end apart: 1, of which 0 were waited for; matrix products, arithmetic and copies ran while one was open for 14% of the time, Pallas kernels for 0%

profile of v1, /device:TPU:0, one launch (start us, length us, event | category | flops | bytes accessed | tf_op | source)
XLA Modules:
  0.0 1050.9 jit_solution(6983654425737057414)
XLA Ops:
  6.5 0.8 copy.296
  7.3 0.7 copy_convert_fusion
  8.1 0.7 maximum_bitcast_fusion
  8.9 3.3 fusion.145
  12.3 8.6 fusion.170
  20.9 5.9 fusion.171
  26.9 5.9 fusion.168
  32.8 5.9 fusion.169
  38.6 5.8 convolution_convert_fusion.14
  44.5 5.9 convolution_convert_fusion.17
  50.3 3.9 copy.314
  54.3 4.1 copy.313
  58.4 10.3 fusion.161
  68.7 17.2 %fusion.201 = (f32[16,512]{1,0:T(8,128)S(1)}, f32[16,512,512]{1,2,0:T(8,128)}) fusion(f32[16,512,512]{1,2,0:T(8,128)} %fusion.161, pred[512,512]{0,1:T(8,128)(4,1)S(1)} %iota_compare_fusion.47), kind=kOutput, calls=%fused_computation.468 | output fusion | flops 25166336 | bytes 33849344 | tf_op jit(solution)/shard_map/sub | solution.py:42
  85.9 9.6 fusion.156
  95.5 28.0 %fusion.200 = (f32[16,512]{1,0:T(8,128)S(1)}, f32[16,512,512]{1,2,0:T(8,128)}) fusion(f32[16,512,512]{1,2,0:T(8,128)} %fusion.156, pred[512,512]{0,1:T(8,128)(4,1)S(1)} %iota_compare_fusion.47), kind=kOutput, calls=%fused_computation.467 | output fusion | flops 25166336 | bytes 33849344 | tf_op jit(solution)/shard_map/sub | solution.py:42
  123.6 7.4 fusion.167
  131.0 7.2 fusion.166
  138.2 0.9 copy-done.2
  139.2 4.9 fusion.155
  144.1 4.7 fusion.154
  148.8 1.0 fusion.134
  149.8 2.3 pad_maximum_fusion
  152.1 2.6 fusion.136
  154.7 1.5 slice.768
  156.1 0.8 fusion.174
  157.9 0.7 reduce_max.27
  159.2 879.7 %conditional.1 = (bf16[2,1,512,2048]{3,2,0,1:T(8,128)(2,1)}) conditional(s32[]{:T(128)} %convert_element_type.265, (s32[2,1,512,6]{2,1,3,0:T(1,128)S(1)}, s32[]{:T(128)}, s32[]{:T(128)}, s32[]{:T(128)}, f32[2,16,2,16,512]{4,3,2,1,0:T(8,128)S(1)}, /*index=5*/s32[]{:T(128)}, bf16[2,512,2048]{2,1,0:T(8,128)(2,1)}, ...), branch_computations={%region_10.19_spmd.clone, %region_19.28_spmd.clone} | conditional | flops 513198144 | bytes 44008048 | solution.py:430
  164.2 0.8 pad.8.homes
  165.0 1.2 copy.309
  170.3 1.5 rev.91
  171.9 1.2 compare_reduce_fusion.8
  173.9 0.7 compare_reduce_fusion.6
  174.7 2.0 fusion.80
  177.0 2.0 fusion.82
  179.5 0.6 copy-done.8
  180.3 0.6 iota_compare_fusion.28
  180.9 0.7 fusion.97
  181.7 0.6 constant_dynamic-update-slice_fusion.47
  182.3 0.6 constant_dynamic-update-slice_fusion.46
  182.9 0.6 constant_dynamic-update-slice_fusion.45
  184.2 0.6 iota_compare_fusion.27
  184.8 0.7 fusion.103
  186.2 0.6 constant_dynamic-update-slice_fusion.42
  186.9 0.6 constant_dynamic-update-slice_fusion.41
  187.5 0.6 constant_dynamic-update-slice_fusion.40.gb
  188.1 850.6 %layer.3 = (bf16[2,512,2048]{2,1,0:T(8,128)(2,1)}, bf16[8,288,2048]{2,1,0:T(8,128)(2,1)}, bf16[8,288,2048]{2,1,0:T(8,128)(2,1)}, bf16[8,288,2048]{2,1,0:T(8,128)...) custom-call(bf16[2,512,2048]{2,1,0:T(8,128)(2,1)} %get-tuple-element, ...), custom_call_target="tpu_custom_call" | custom-call | tf_op jit(solution)/shard_map/cond/branch_1_fun/layer/pallas_call | solution.py:402
  1038.9 4.8 copy.423
  (140 shorter events, 8.9 us)
Async XLA Ops:
  6.5 5.7 copy-start.13
  6.5 148.1 %all-gather.3.cloned.1.call-start = ((), (), s32[]{:S(2)}) async-start(), calls=%async_computation | async-start | bytes 2162688 | tf_op jit(solution)/shard_map/all_gather | solution.py:349
  8.8 3.5 copy-start.1
  8.9 11.9 %slice-start.2 = ((s8[8388608]{0:T(1024)(128)(4,1)}), s8[4194304]{0:T(1024)(128)(4,1)S(1)}, s32[]{:S(2)}) async-start(s8[8388608]{0:T(1024)(128)(4,1)} %bitcast.486), calls=%async_computation.3 | async-start | bytes 8388608
  12.3 8.6 slice-start.3
  12.3 14.6 %slice-start = ((s8[8388608]{0:T(1024)(128)(4,1)}), s8[4194304]{0:T(1024)(128)(4,1)S(1)}, s32[]{:S(2)}) async-start(s8[8388608]{0:T(1024)(128)(4,1)} %bitcast.484), calls=%async_computation.1 | async-start | bytes 8388608
  20.9 6.0 slice-start.1
  26.9 11.8 %slice-start.4 = ((s8[8388608]{0:T(1024)(128)(4,1)}), s8[4194304]{0:T(1024)(128)(4,1)S(1)}, s32[]{:S(2)}) async-start(s8[8388608]{0:T(1024)(128)(4,1)} %bitcast.488), calls=%async_computation.5 | async-start | bytes 8388608
  32.8 5.9 slice-start.5
  95.5 28.0 %copy-start.4 = (bf16[512,2048]{0,1:T(8,128)(2,1)S(1)}, bf16[512,2048]{0,1:T(8,128)(2,1)}, u32[]{:S(2)}) copy-start(bf16[512,2048]{0,1:T(8,128)(2,1)} %copy.313) | copy-start | bytes 6291460
  123.6 7.4 copy-start.3
  123.6 14.7 %slice-start.6 = ((s8[8388608]{0:T(1024)(128)(4,1)}), s8[4194304]{0:T(1024)(128)(4,1)S(1)}, s32[]{:S(2)}) async-start(s8[8388608]{0:T(1024)(128)(4,1)} %bitcast.490), calls=%async_computation.7 | async-start | bytes 8388608
  131.0 7.3 slice-start.7
  131.0 8.2 copy-start.2
  149.8 2.3 copy-start.12
  154.7 4.5 copy-start.9
  154.7 4.5 copy-start
  163.9 2.5 copy-start.10
  179.5 0.7 copy-start.8
  180.3 5.4 copy-start.7
Sparse Core Ops, SparseCore 0:
  10.2 58.9 all-gather.2

commit v2 on v1

--- a/solution.py
+++ b/solution.py
@@ -10,7 +10,7 @@
 HEAD = 128
 LANES = 128
 TILE = 128
-WIDTH = 288
+WIDTH, WINDOW = 288, 208
 NONE = -(1 << 20)
 F32, BF16, I32 = jnp.float32, jnp.bfloat16, jnp.int32
 ANY = pl.BlockSpec(memory_space=pl.ANY)
@@ -68,17 +68,32 @@
     return idx[:, :, None, :] == e[None, None, :, None]
 
 
-def layer_kernel(cap, steps, z, h, lists, homes, px, pb, gb, w1, w3, w2,
-                 y, ls, za, zy, zk, eo, em, ei, po, pm, pi, sr, rr,
-                 zin, zb, x, act, w13b, w2b, ob, lsem, wsem, send, recv, ksend, krecv):
+def list_kernel(pos, z, *outs):
+    width, d = outs[0].shape
+    row = lax.broadcasted_iota(I32, (width, z.shape[0]), 0)
+    for l, o in enumerate(outs):
+        sel = jnp.where(row == pos[l:l + 1, :], 1.0, 0.0).astype(BF16)
+        for c in range(4):
+            cols = slice(c * d // 4, (c + 1) * d // 4)
+            o[:, cols] = jnp.dot(sel, z[:, cols], preferred_element_type=F32).astype(BF16)
+
+
+def layer_kernel(cap, steps, z0, z1, h0, h1, lists, homes, px, pb, gb, w1, w3, w2,
+                 y, ls, z2, zy, zk, eo, em, ei, po, pm, pi, sr, rr,
+                 zin, zb, x, act, w13b, w2b, ob, lsem, psem, wsem, send, recv, ksend, krecv):
     el, d, f = w1.shape
-    nm, t, _ = z.shape
+    t, _ = z1.shape
+    h = (h0, h1)
+    nm = len(h)
     nb = steps * nm
-    width = zb.shape[1]
+    width, window = zb.shape[1], zy.shape[1]
+    gap = width - window
     rows = el * cap
     fb = f // LANES
     quarter = d // 4
     dp, row, col = lax.axis_index("dp"), lax.axis_index("row"), lax.axis_index("col")
+    near = pl.ds(pl.multiple_of(gap * (col // 2), 16), window)
+    far = pl.ds(pl.multiple_of(gap * (1 - col // 2), 16), window)
     core = (dp, row, col + 1 - 2 * lax.rem(col, 2))
     chip = (dp, row, col + 2 - 4 * (col // 2))
 
@@ -94,15 +109,40 @@
         return pltpu.make_async_remote_copy(src_ref=src.at[n], dst_ref=dst.at[n], send_sem=send.at[kind, n],
                                             recv_sem=recv.at[kind, n], device_id=device, device_id_type=MESH)
 
+    def pair(src, dst, send_sem, recv_sem, device):
+        return pltpu.make_async_remote_copy(src_ref=src, dst_ref=dst, send_sem=send_sem, recv_sem=recv_sem,
+                                            device_id=device, device_id_type=MESH)
+
+    def by_half(n, act_on):
+        if isinstance(n, int):
+            act_on(z0.at[n] if n < steps else z2.at[n - steps])
+            return
+
+        @pl.when(n < steps)
+        def _():
+            act_on(z0.at[n])
+
+        @pl.when(n >= steps)
+        def _():
+            act_on(z2.at[n - steps])
+
     def go_row(n):
-        return remote(ls, za, 0, n, other(step_of(n)))
-
-    def go_chip(n):
-        return remote(za, zy, 1, n, chip)
-
-    def go_core(n, i):
-        return pltpu.make_async_remote_copy(src_ref=(zy, za)[i].at[n], dst_ref=zk.at[n, i], send_sem=ksend.at[n, i],
-                                            recv_sem=krecv.at[n, i], device_id=core, device_id_type=MESH)
+        return pair(ls.at[n - steps], z2.at[n - steps], send.at[0, n], recv.at[0, n], other(step_of(n)))
+
+    def go_chip(n, src=None):
+        src = z0.at[0] if src is None else src
+        return pair(src.at[far], zy.at[n], send.at[1, n], recv.at[1, n], chip)
+
+    def start_chip(n):
+        by_half(n, lambda src: go_chip(n, src).start())
+
+    def go_core(n, i, src=None):
+        src = zy.at[n] if i == 0 else (z0.at[0] if src is None else src).at[near]
+        return pair(src, zk.at[n, i], ksend.at[n, i], krecv.at[n, i], core)
+
+    def start_core(n):
+        go_core(n, 0).start()
+        by_half(n, lambda src: go_core(n, 1, src).start())
 
     def go_expert(n):
         return remote(eo, ei, 2, n, core)
@@ -144,63 +184,60 @@
             c.start()
     pl.semaphore_wait(barrier, len(partners))
 
-    for m in range(nm):
-        run(local(z.at[m], zin, 0))
-        for i, r in enumerate(STEPS[m]):
-            n = m * steps + i
-            put = local(zb.at[i % 2], (za if r == 0 else ls).at[n], 1 + i % 2)
-            sel = jnp.where(hot(lists[m, r:r + 1, :], width), 1.0, 0.0).astype(BF16)
-            for c in range(4):
-                cols = slice(c * quarter, (c + 1) * quarter)
-                zb[i % 2, :, cols] = jnp.dot(sel, zin[:, cols], preferred_element_type=F32).astype(BF16)
-            run(put)
-            if r:
-                go_row(n).start()
-            elif m == 0:
-                go_chip(n).start()
-
-    go_row(1).wait_recv()
-    go_chip(1).start()
-    go_chip(0).wait_recv()
-    for i in range(2):
-        go_core(0, i).start()
+    start_chip(0)
+    run(local(z1, zin, 0))
+    for i, r in enumerate(STEPS[1]):
+        n = steps + i
+        put = local(zb.at[i % 2], (z2 if r == 0 else ls).at[i], 1 + i % 2)
+        sel = jnp.where(hot(lists[r:r + 1, :], width), 1.0, 0.0).astype(BF16)
+        for c in range(4):
+            cols = slice(c * quarter, (c + 1) * quarter)
+            zb[i % 2, :, cols] = jnp.dot(sel, zin[:, cols], preferred_element_type=F32).astype(BF16)
+        run(put)
+        if r:
+            go_row(n).start()
+        if i == 0:
+            go_chip(0).wait_recv()
+            start_core(0)
+            start_chip(1)
 
     def dispatch(n):
         @pl.when(n + 1 < nb)
         def _():
             go_chip(n + 1).wait_recv()
-            for i in range(2):
-                go_core(n + 1, i).start()
+            start_core(n + 1)
 
         @pl.when(n + 2 < nb)
         def _():
-            @pl.when(step_of(n + 2) != 0)
+            @pl.when(jnp.logical_and(n + 2 >= steps, step_of(n + 2) != 0))
             def _():
                 go_row(n + 2).wait_recv()
-            go_chip(n + 2).start()
+            start_chip(n + 2)
 
     def experts(n):
         for i in range(2):
             go_core(n, i).wait_recv()
-        srcs = (zk.at[n, 0], zk.at[n, 1], zy.at[n], za.at[n])
-        fetch = lambda i: local(srcs[i], zb.at[i % 2], 1 + i % 2)
-        fetch(0).start()
+        srcs = (zk.at[n, 0], zk.at[n, 1], zy.at[n])
+        fetch = lambda i, src: local(src, zb.at[i % 2, pl.ds(0, window)], 1 + i % 2)
+        fetch(0, srcs[0]).start()
         for i in range(4):
-            if i + 1 < 4:
-                fetch(i + 1).start()
-            fetch(i).wait()
+            if i + 1 < 3:
+                fetch(i + 1, srcs[i + 1]).start()
+            elif i + 1 == 3:
+                by_half(n, lambda src: fetch(3, src.at[near]).start())
+            fetch(i, srcs[min(i, 2)]).wait()
             sel = jnp.concatenate([jnp.where(hot(px[n, i * el + e:i * el + e + 1, :], cap), 1.0, 0.0).astype(BF16)
                                    for e in range(el)], 0)
             for c in range(4):
                 cols = slice(c * quarter, (c + 1) * quarter)
-                v = jnp.dot(sel, zb[i % 2, :, cols], preferred_element_type=F32).astype(BF16)
+                v = jnp.dot(sel, zb[i % 2, 0:window, cols], preferred_element_type=F32).astype(BF16)
                 for e in range(el):
                     x[e * rows + i * cap:e * rows + (i + 1) * cap, cols] = v[e * cap:(e + 1) * cap]
 
         def put(e, i):
             return pltpu.make_async_copy(x.at[pl.ds(pl.multiple_of(e * rows + i * cap, 32), cap)],
                                          (eo if i < 2 else em).at[n, i % 2, pl.ds(pl.multiple_of(e * cap, 32), cap)],
-                                         lsem.at[3 + i])
+                                         psem.at[e, i])
 
         def expert(e, carry):
             s = lax.rem(e, 2)
@@ -217,7 +254,8 @@
                     x[at, cols] = jnp.dot(act[...], w2b[s, :, cols], preferred_element_type=F32).astype(BF16)
                 return cc
             lax.fori_loop(0, rows // TILE, tile, 0)
-            run(*[put(e, i) for i in range(4)])
+            for i in range(4):
+                put(e, i).start()
 
             @pl.when(n * el + e + 2 < nb * el)
             def _():
@@ -225,6 +263,9 @@
                     c.start()
             return carry
         lax.fori_loop(0, el, expert, 0)
+        for e in range(el):
+            for i in range(4):
+                put(e, i).wait()
         go_expert(n).start()
 
     def combine(n):
@@ -245,8 +286,8 @@
                 cols = slice(c * quarter, (c + 1) * quarter)
                 b = x[2 * i * rows:2 * (i + 1) * rows, cols]
                 a = [lax.dot_general(p, b, (((0,), (0,)), ((), ())), preferred_element_type=F32) for p in parts]
-                ob[i, :, cols] = a[0] + a[1] + a[2]
-            put = local(ob.at[i], (po, pm)[i].at[n], 5 + i)
+                ob[i, 0:window, cols] = a[0] + a[1] + a[2]
+            put = local(ob.at[i, pl.ds(0, window)], (po, pm)[i].at[n], 5 + i)
             put.start()
             if i == 0:
                 put.wait()
@@ -257,35 +298,36 @@
     def forward(n):
         go_part(n).wait_recv()
 
+        copies = (local(pm.at[n], ob.at[0, near], 1), local(pi.at[n], ob.at[1, far], 2))
+        for c in copies:
+            c.start()
+        if gap:
+            for i, first in enumerate((1 - col // 2, col // 2)):
+                ob[i, pl.ds(pl.multiple_of(window * first, 16), gap), :] = jnp.zeros((gap, d), F32)
+        for c in copies:
+            c.wait()
+        ob[0] = ob[0] + ob[1]
+        run(local(ob.at[0], sr.at[n], 1))
+
         @pl.when(step_of(n) != 0)
         def _():
-            run(local(pm.at[n], ob.at[0], 1), local(pi.at[n], ob.at[1], 2))
-            ob[0] = ob[0] + ob[1]
-            run(local(ob.at[0], sr.at[n], 1))
             go_sum(n).start()
 
     def finish(m):
         at = [m * steps + STEPS[m].index(r) for r in range(steps)]
         for r in range(1, steps):
             go_sum(at[r]).wait_recv()
-        refs = [pm.at[at[0]], pi.at[at[0]]] + [rr.at[at[r]] for r in range(1, steps)]
+        refs = [sr.at[at[0]]] + [rr.at[at[r]] for r in range(1, steps)]
         lane = lax.broadcasted_iota(I32, (t, width), 1)
-        fill = local(h.at[m], zin, 0)
-        fill.start()
-        fill.wait()
+        run(local(h[m], zin, 0))
         for c in range(4):
             cols = slice(c * quarter, (c + 1) * quarter)
-            spot = lambda l: ob.at[l // 4, :, pl.ds(l % 4 * quarter, quarter)]
+            spot = lambda l: ob.at[0, :, pl.ds(l * quarter, quarter)]
             run(*[local(a.at[:, pl.ds(c * quarter, quarter)], spot(l), 1 + l) for l, a in enumerate(refs)])
             v = zin[:, cols].astype(F32)
             for r in range(steps):
                 one = jnp.where(lane == homes[m, :, r:r + 1], 1.0, 0.0).astype(BF16)
-                if r == 0:
-                    u = ob[0, :, 0:quarter] + ob[0, :, quarter:2 * quarter]
-                else:
-                    l = r + 1
-                    u = ob[l // 4, :, l % 4 * quarter:(l % 4 + 1) * quarter]
-                for p in split3(u):
+                for p in split3(ob[0, :, r * quarter:(r + 1) * quarter]):
                     v = v + jnp.dot(one, p, preferred_element_type=F32)
             zin[:, cols] = v.astype(BF16)
         run(local(zin, y.at[m], 0))
@@ -320,8 +362,11 @@
 
         @pl.when(step_of(n) != 0)
         def _():
-            go_row(n).wait_send()
             go_sum(n).wait_send()
+
+            @pl.when(n >= steps)
+            def _():
+                go_row(n).wait_send()
         return carry
     lax.fori_loop(0, nb, drain, 0)
 
@@ -349,12 +394,24 @@
         every = lax.all_gather(pay, tok_axes)
         every = every.reshape((-1, ep) + every.shape[1:])
 
-        def width_needed():
-            rows_of = every[:, :, :, :top] // layer
-            hit = jnp.any(rows_of[..., None] == jnp.arange(nrow, dtype=F32), axis=3)
-            return jnp.max(jnp.sum(hit.astype(I32), axis=3))
-
-        need = width_needed()
+        def halves(idx_, first):
+            half = layer // 2
+            return [jnp.any(idx_ // half == 2 * first + c, -2) for c in range(2)]
+
+        def width_needed(gap):
+            need = 0
+            for r in range(nrow):
+                a, b = halves(every[:, :, :, :top].astype(I32), r)
+                na, nb, both = (jnp.sum(v.astype(I32), -1) for v in (a & ~b, b & ~a, a & b))
+                need = jnp.maximum(need, jnp.max(jnp.maximum(na, gap) + both + jnp.maximum(nb, gap)))
+            return need
+
+        def places_of(a, b, gap, width):
+            only = [ranks(v) for v in (a & ~b, a & b, b & ~a)]
+            na = jnp.sum((a & ~b).astype(I32), -1, keepdims=True)
+            mid = jnp.maximum(na, gap)
+            return jnp.where(a & b, mid + only[1], jnp.where(a, only[0], jnp.where(b, width - 1 - only[2], NONE)))
+
         mine = lax.dynamic_index_in_dim(every, lax.axis_index("dp"), 0, keepdims=False)
 
         def flip(a, axis, bit):
@@ -365,11 +422,12 @@
             a = jnp.flip(lax.dynamic_slice_in_dim(jnp.concatenate([a, a]), row + 1, nrow), 0)
             return flip(flip(jnp.swapaxes(a, 1, 2), 1, core), 2, chip)
 
-        def lists_of(m):
+        def lists_of(m, width, window):
             steps = lax.rem(row + jnp.arange(nrow, dtype=I32), nrow)
-            return ranks(jnp.any(idx[m].reshape(1, t, top) // layer == steps[:, None, None], 2))
-
-        def routes(m, width):
+            own = jnp.broadcast_to(idx[m].reshape(t, top).T[None], (nrow, top, t))
+            return places_of(*halves(own, steps[:, None, None]), width - window, width)
+
+        def routes(m, width, window):
             ia = relative(mine[:, m, :top].astype(I32)).reshape(ep, top, t)
             ga = relative(mine[:, m, top:2 * top])[:, 1].reshape(ep // 2, top, t)
             own = lambda a: a.reshape((nrow, 2, 2) + a.shape[1:])[:, 1].reshape((ep // 2,) + a.shape[1:])
@@ -377,33 +435,45 @@
             hits = among(ia, k * (me // 2), k)
             pos = ranks(jnp.any(hits, 1))
             g = jnp.sum(jnp.where(own(hits), ga[:, :, None, :], 0.0), 1)
-            listed = ranks(jnp.any(ia // layer == row, 1))
-            lists = (listed[:, :, None] == jnp.arange(width, dtype=I32)).astype(BF16)
+            listed = places_of(*halves(ia, row), width - window, width) - chip * (width - window)
+            lists = (listed[:, :, None] == jnp.arange(window, dtype=I32)).astype(BF16)
             places = jnp.einsum("pet,ptc->pec", (jnp.maximum(pos, -1) + 1).astype(BF16), lists,
                                 preferred_element_type=F32).astype(I32) - 1
             gs = jnp.einsum("pet,ptc->pec", jnp.concatenate(split3(g), 1), own(lists), preferred_element_type=F32)
             lgate = gs[:, :k] + gs[:, k:2 * k] + gs[:, 2 * k:]
             turn = lambda a: jnp.where(core == 0, a, jnp.roll(a, el, axis=1))
             places = turn(places)
-            lpos = own(places).reshape(nrow, 2 * k, width)
-            lgate = turn(lgate).reshape(nrow, 2 * k, width)
-            return places[:, :el].reshape(nrow, 4 * el, width), lpos, lgate
-
-        def layers(width, zs, hs):
-            lists = jnp.stack([lists_of(m) for m in range(nm)])
-            homes = jnp.pad(jnp.swapaxes(lists, 1, 2), ((0, 0), (0, 0), (0, LANES - nrow)))
-            rt = [routes(m, width) for m in range(nm)]
+            lpos = own(places).reshape(nrow, 2 * k, window)
+            lgate = turn(lgate).reshape(nrow, 2 * k, window)
+            return places[:, :el].reshape(nrow, 4 * el, window), lpos, lgate
+
+        def layers(width, window, z0, h0, x):
+            lists = [lists_of(m, width, window) for m in range(nm)]
+            out = jax.ShapeDtypeStruct((width, d), BF16)
+            rows0 = pl.pallas_call(
+                list_kernel, out_shape=[out] * nrow, in_specs=[VMEM, VMEM], out_specs=[VMEM] * nrow, name="lists",
+                compiler_params=pltpu.CompilerParams(vmem_limit_bytes=67043328),
+                cost_estimate=pl.CostEstimate(flops=50_000_000, bytes_accessed=7_000_000, transcendentals=0),
+            )(lists[0], z0)
+            came = jnp.stack([rows0[r] if r == 0 else lax.ppermute(rows0[r], "row", [(i, (i + r) % nrow) for i in range(nrow)])
+                              for r in STEPS[0]])
+            x1, _ = lax.optimization_barrier((x[1], rows0[0]))
+            h1 = attention(x1, wq, wk, wv, wo, gattn)
+            z1 = rms(h1, gmoe)
+            homes = jnp.stack([jnp.pad(a.T, ((0, 0), (0, LANES - nrow))) for a in lists])
+            rt = [routes(m, width, window) for m in range(nm)]
             px, pb, gb = (jnp.concatenate([jnp.stack([rt[m][k][r] for r in STEPS[m]]) for m in range(nm)]) for k in range(3))
             nb = nm * nrow
             rows = el * cap
-            wide = jax.ShapeDtypeStruct((nb, width, d), BF16)
+            wide = jax.ShapeDtypeStruct((nrow, width, d), BF16)
+            part = jax.ShapeDtypeStruct((nb, window, d), F32)
             exact = jax.ShapeDtypeStruct((nb, width, d), F32)
             pair = jax.ShapeDtypeStruct((nb, 2, rows, d), BF16)
             y, *_ = pl.pallas_call(
                 functools.partial(layer_kernel, cap, nrow),
-                out_shape=[jax.ShapeDtypeStruct((nm, t, d), BF16), wide, wide, wide,
-                           jax.ShapeDtypeStruct((nb, 2, width, d), BF16), pair, pair, pair] + [exact] * 5,
-                in_specs=[ANY] * 2 + [VMEM] * 5 + [ANY] * 3, out_specs=[ANY] * 13,
+                out_shape=[jax.ShapeDtypeStruct((nm, t, d), BF16), wide, wide, jax.ShapeDtypeStruct((nb, window, d), BF16),
+                           jax.ShapeDtypeStruct((nb, 2, window, d), BF16), pair, pair, pair] + [part] * 3 + [exact] * 2,
+                in_specs=[ANY] * 4 + [VMEM] * 5 + [ANY] * 3, out_specs=[ANY] * 13,
                 scratch_shapes=[
                     pltpu.VMEM((t, d), BF16),
                     pltpu.VMEM((2, width, d), BF16),
@@ -413,6 +483,7 @@
                     pltpu.VMEM((2, f, d), BF16),
                     pltpu.VMEM((2, width, d), F32),
                     pltpu.SemaphoreType.DMA((8,)),
+                    pltpu.SemaphoreType.DMA((el, 4)),
                     pltpu.SemaphoreType.DMA((2, 2 * (f // LANES) + 1)),
                     pltpu.SemaphoreType.DMA((5, nb)),
                     pltpu.SemaphoreType.DMA((5, nb)),
@@ -422,12 +493,13 @@
                 compiler_params=pltpu.CompilerParams(vmem_limit_bytes=67043328, has_side_effects=True,
                                                      collective_id=0 if width < t else 1),
                 name="layer",
-            )(zs, hs, lists, homes, px, pb, gb, w1, w3, w2)
+            )(came, z1, h0, h1, lists[1], homes, px, pb, gb, w1, w3, w2)
             return y.reshape(nm, ns, seq, d)
 
-        hs = jnp.stack([attention(x[m], wq, wk, wv, wo, gattn) for m in range(nm)])
-        zs = rms(hs, gmoe)
-        return lax.cond(need <= WIDTH, functools.partial(layers, WIDTH), functools.partial(layers, t), zs, hs)
+        h0 = attention(x[0], wq, wk, wv, wo, gattn)
+        z0 = rms(h0, gmoe)
+        fits = width_needed(WIDTH - WINDOW) <= WIDTH
+        return lax.cond(fits, functools.partial(layers, WIDTH, WINDOW), functools.partial(layers, t, t), z0, h0, x)
 
     tok_spec = P(None, tok_axes)
     exp_spec = P(ep_axes)

time: 1060 us -> 964 us (0.909)
  Pallas kernels: 851 us -> 698 us
  matrix products: 88.2 us -> 109 us
  loops' own time: 5.05 us -> 19.3 us
  other arithmetic: 63.6 us -> 74.5 us
    pallas_call x1, Pallas kernels: 851 us -> 693 us  [layers(): pl.pallas_call(functools.partial(layer_kernel, cap, nrow), out_shape=[jax...]
    another operation x1, loops' own time: 5.05 us -> 19.3 us  [local(): lax.cond(fits, functools.partial(layers, WIDTH, WINDOW), functools.partia...]
  transfers between devices with their start and end apart: 1 -> 4, of which waited for: 0 -> 0; matrix products, arithmetic and copies ran while one was open for 14% -> 19% of each run, Pallas kernels for 0% -> 0%
where the time goes in v2:
time: 964 us; the launch traced here: 958 us
  Pallas kernels  698 us (72%)
  matrix products  109 us (11%)
  other arithmetic  74.5 us (8%)
  local copies, waits for them, and re-layouts  34.3 us (4%)
  loops' own time  19.3 us (2%)
  between operations  16.5 us (2%)
    pallas_call x1, Pallas kernels, layers(): pl.pallas_call(functools.partial(layer_kernel, cap, nrow), out_shape=[jax...  693 us
    dot_general x6, matrix products, proj(): a = jnp.dot(u, w, preferred_element_type=F32).astype(BF16)  42.3 us
    sub x2, other arithmetic, attention(): p = jax.nn.softmax(s, axis=-1).astype(BF16)  35 us
    dot_general x2, matrix products, attention(): jnp.einsum('bqhe,bkhe->bhqk', q, k, preferred_element_type=F32)  20 us
    another operation x1, loops' own time, local(): lax.cond(fits, functools.partial(layers, WIDTH, WINDOW), functools.partia...  19.3 us
  transfers between devices with their start and end apart: 4, of which 0 were waited for; matrix products, arithmetic and copies ran while one was open for 19% of the time, Pallas kernels for 0%

profile of v2, /device:TPU:0, one launch (start us, length us, event | category | flops | bytes accessed | tf_op | source)
XLA Modules:
  0.0 958.3 jit_solution(14665692953910413219)
XLA Ops:
  8.9 2.2 fusion.279
  11.2 8.7 fusion.289
  20.0 6.1 fusion.290
  26.1 5.8 convolution_convert_fusion.36
  31.9 3.9 copy.745
  35.8 9.7 %fusion.283 = f32[16,512,512]{1,2,0:T(8,128)} fusion(bf16[64,16,8,128]{3,2,1,0:T(8,128)(2,1)} %fusion.290, bf16[64,16,8,128]{3,2,1,0:T(8,128)(2,1)S(1)} %fusion.289), kind=kOutput, calls=%fused_computation.650 | convolution fusion | flops 1073741824 | bytes 20971520 | tf_op jit(solution)/shard_map/bqhe,bkhe->bhqk/dot_general | solution.py:40
  45.5 17.7 %fusion.330 = (f32[16,512]{1,0:T(8,128)S(1)}, f32[16,512,512]{1,2,0:T(8,128)}) fusion(f32[16,512,512]{1,2,0:T(8,128)} %fusion.283, pred[512,512]{0,1:T(8,128)(4,1)S(1)} %iota_compare_fusion.64), kind=kOutput, calls=%fused_computation.725 | output fusion | flops 25166336 | bytes 33849344 | tf_op jit(solution)/shard_map/sub | solution.py:42
  63.2 7.4 fusion.288
  70.6 8.9 fusion.276
  79.5 1.3 copy-done
  80.8 1.9 fusion.278
  82.7 5.2 compare_reduce_fusion.13
  87.9 3.3 fusion.299
  91.7 3.3 fusion.293
  100.5 845.7 %conditional.1 = (bf16[2,1,512,2048]{3,2,0,1:T(8,128)(2,1)}) conditional(s32[]{:T(128)} %convert_element_type.517, (s32[2,1,512,6]{2,1,3,0:T(1,128)S(1)}, s32[]{:T(128)}, bf16[512,2048]{1,0:T(8,128)(2,1)}, bf16[2,1,512,2048]{3,2,1,0:T(8,128)(2,1)}, f32[2048]{0:T(1024)}, /*index=5*/bf16[2048,2048]{1,0:T(8,128)(2,1)}, bf16[2048,2048]{1,0:T(8,128)(2,1)}, ...), branch_computations={%region_28.49_spmd, %region_49.70_spmd} | conditional | flops 20012308480 | bytes 309304448 | solution.py:502
  120.0 1.1 convert_reduce_fusion.3
  121.4 1.1 select_select_fusion.3
  123.2 5.2 lists.3
  128.5 3.1 collective-permute-start.3
  131.5 2.0 collective-permute-start.4
  133.6 1.0 collective-permute-start.5
  134.7 0.9 copy.660
  135.5 0.9 copy.661
  136.4 1.1 convolution_convert_fusion.24
  137.5 1.1 convert_reduce_fusion.2
  138.6 2.8 copy.718
  152.0 1.3 select_select_fusion.2
  154.0 1.2 fusion.194
  155.3 1.1 fusion.199
  156.5 1.7 slice_bitcast_fusion.19
  162.1 2.3 fusion.172
  164.3 2.3 fusion.171
  170.6 1.2 iota_compare_fusion.36
  171.8 1.5 fusion.219
  173.3 1.2 iota_compare_fusion.37
  174.4 1.5 fusion.213
  176.6 9.5 fusion.157
  186.2 6.3 fusion.158
  192.5 5.8 convolution_convert_fusion.19
  198.3 4.0 copy.740
  203.3 10.3 %fusion.151 = f32[16,512,512]{1,2,0:T(8,128)} fusion(bf16[64,16,8,128]{3,2,1,0:T(8,128)(2,1)} %fusion.158, bf16[64,16,8,128]{3,2,1,0:T(8,128)(2,1)} %fusion.157), kind=kOutput, calls=%fused_computation.345 | convolution fusion | flops 1073741824 | bytes 20971520 | tf_op jit(solution)/shard_map/cond/branch_1_fun/bqhe,bkhe->bhqk/dot_general | solution.py:40
  213.6 17.2 %fusion.329 = (f32[16,512]{1,0:T(8,128)S(1)}, f32[16,512,512]{1,2,0:T(8,128)}) fusion(f32[16,512,512]{1,2,0:T(8,128)} %fusion.151, pred[512,512]{0,1:T(8,128)(4,1)S(1)} %iota_compare_fusion.46), kind=kOutput, calls=%fused_computation.724 | output fusion | flops 25166336 | bytes 33849344 | tf_op jit(solution)/shard_map/cond/branch_1_fun/sub | solution.py:42
  230.9 7.7 fusion.156
  238.6 8.6 fusion.142
  247.2 1.9 fusion.144.z1
  249.3 3.8 pad_maximum_fusion.1.z0
  253.1 692.8 %layer.3 = (bf16[2,512,2048]{2,1,0:T(8,128)(2,1)}, bf16[4,288,2048]{2,1,0:T(8,128)(2,1)}, bf16[4,288,2048]{2,1,0:T(8,128)(2,1)}, bf16[8,208,2048]{2,1,0:T(8,128)...) custom-call(bf16[4,288,2048]{2,1,0:T(8,128)(2,1)} %pad_maximum_fusio, ...), custom_call_target="tpu_custom_call" | custom-call | tf_op jit(solution)/shard_map/cond/branch_1_fun/layer/pallas_call | solution.py:472
  946.2 4.8 copy.862
  (249 shorter events, 28.9 us)
Async XLA Ops:
  6.5 76.1 %all-gather.3.cloned.1.call-start = ((), (), s32[]{:S(2)}) async-start(), calls=%async_computation | async-start | bytes 2162688 | tf_op jit(solution)/shard_map/all_gather | solution.py:394
  8.9 11.0 %slice-start.6 = ((s8[8388608]{0:T(1024)(128)(4,1)}), s8[4194304]{0:T(1024)(128)(4,1)S(1)}, s32[]{:S(2)}) async-start(s8[8388608]{0:T(1024)(128)(4,1)} %bitcast.715), calls=%async_computation.7 | async-start | bytes 8388608
  11.2 8.8 copy-start.1
  11.2 8.8 slice-start.7
  11.2 8.8 copy-start.56
  11.2 14.9 %slice-start = ((s8[8388608]{0:T(1024)(128)(4,1)}), s8[4194304]{0:T(1024)(128)(4,1)S(1)}, s32[]{:S(2)}) async-start(s8[8388608]{0:T(1024)(128)(4,1)} %bitcast.709), calls=%async_computation.1 | async-start | bytes 8388608
  20.0 6.1 slice-start.1
  45.5 17.7 %copy-start.5 = (bf16[512,2048]{0,1:T(8,128)(2,1)S(1)}, bf16[512,2048]{0,1:T(8,128)(2,1)}, u32[]{:S(2)}) copy-start(bf16[512,2048]{0,1:T(8,128)(2,1)} %copy.745) | copy-start | bytes 6291460
  63.2 7.4 copy-start.2
  70.6 10.2 %copy-start.37 = (f32[2048]{0:T(1024)S(1)}, f32[2048]{0:T(1024)}, u32[]{:S(2)}) copy-start(f32[2048]{0:T(1024)} %param.22) | copy-start | bytes 24580
  79.5 1.3 copy-start
  79.5 21.0 %copy-start.29 = (s32[2,1,512,6]{2,1,3,0:T(1,128)S(1)}, s32[2,1,512,6]{2,1,3,0:T(1,128)}, u32[]{:S(2)}) copy-start(s32[2,1,512,6]{2,1,3,0:T(1,128)} %param.15) | copy-start | bytes 73732
  119.4 2.0 copy-start.11
  119.6 2.9 copy-start.13
  120.0 3.2 copy-start.20
  121.1 2.1 copy-start.52
  128.5 120.6 %collective-permute-start.3 = (bf16[288,2048]{1,0:T(8,128)(2,1)}, bf16[288,2048]{1,0:T(8,128)(2,1)}, u32[]{:S(2)}, u32[]{:S(2)}) collective-permute-start(bf16[288,2048]{1,0:T(8,128)(2,1)} %get-tuple-element.108), channel_id=1, source_target_pairs={{0,4},{4,8},{8,12},{12,0},{1,5},{5,9},{9,13},{13,1},{2,6},{6,10},{... | collective-permute-start | bytes 3538952 | tf_op jit(solution)/shard_map/cond/branch_1_fun/ppermute | solution.py:458
  131.5 117.5 %collective-permute-start.4 = (bf16[288,2048]{1,0:T(8,128)(2,1)}, bf16[288,2048]{1,0:T(8,128)(2,1)}, u32[]{:S(2)}, u32[]{:S(2)}) collective-permute-start(bf16[288,2048]{1,0:T(8,128)(2,1)} %get-tuple-element.109), channel_id=1, source_target_pairs={{0,12},{4,0},{8,4},{12,8},{1,13},{5,1},{9,5},{13,9},{2,14},{6,2},{... | collective-permute-start | bytes 3538952 | tf_op jit(solution)/shard_map/cond/branch_1_fun/ppermute | solution.py:458
  133.6 115.5 %collective-permute-start.5 = (bf16[288,2048]{1,0:T(8,128)(2,1)}, bf16[288,2048]{1,0:T(8,128)(2,1)}, u32[]{:S(2)}, u32[]{:S(2)}) collective-permute-start(bf16[288,2048]{1,0:T(8,128)(2,1)} %get-tuple-element.110), channel_id=1, source_target_pairs={{0,8},{4,12},{8,0},{12,4},{1,9},{5,13},{9,1},{13,5},{2,10},{6,14},... | collective-permute-start | bytes 3538952 | tf_op jit(solution)/shard_map/cond/branch_1_fun/ppermute | solution.py:458
  146.2 5.6 copy-start.48
  148.2 7.1 copy-start.12
  148.2 7.1 copy-start.14
  148.2 7.1 copy-start.21
  148.2 7.1 copy-start.22
  148.2 7.1 copy-start.53
  159.1 2.2 copy-start.46
  160.7 0.6 copy-start.47
  168.1 6.3 copy-start.31
  171.7 4.9 copy-start.58
  176.1 10.1 %slice-start.10 = ((s8[8388608]{0:T(1024)(128)(4,1)}), s8[4194304]{0:T(1024)(128)(4,1)S(1)}, s32[]{:S(2)}) async-start(s8[8388608]{0:T(1024)(128)(4,1)} %bitcast.719), calls=%async_computation.11 | async-start | bytes 8388608 | tf_op jit(solution)/shard_map/cond
  176.6 9.6 slice-start.11
  176.6 15.8 %slice-start.4 = ((s8[8388608]{0:T(1024)(128)(4,1)}), s8[4194304]{0:T(1024)(128)(4,1)S(1)}, s32[]{:S(2)}) async-start(s8[8388608]{0:T(1024)(128)(4,1)} %bitcast.713), calls=%async_computation.5 | async-start | bytes 8388608 | tf_op jit(solution)/shard_map/cond
  186.2 6.3 slice-start.5
  198.3 4.8 copy-start.41
  198.3 4.8 copy-start.40
  198.3 4.9 copy-start.45
  198.3 4.9 copy-start.44
  198.3 4.9 copy-start.43
  198.3 4.9 copy-start.42
  203.3 10.3 %copy-start.30 = (s32[8,16,208]{2,1,0:T(8,128)}, s32[8,16,208]{2,1,0:T(8,128)S(1)}, u32[]{:S(2)}) copy-start(s32[8,16,208]{2,1,0:T(8,128)S(1)} %constant_dynamic-update-slice_fusion.24.px) | copy-start | bytes 319492 | tf_op jit(solution)/shard_map/cond
  238.6 8.7 copy-start.39
  247.2 6.0 copy-start.4
  247.2 2.1 copy-start.7
  247.2 5.9 copy-start.32
Sparse Core Ops, SparseCore 0:
  10.2 58.9 all-gather.2

commit v3 on v2

--- a/solution.py
+++ b/solution.py
@@ -9,7 +9,7 @@
 
 HEAD = 128
 LANES = 128
-TILE = 128
+TILE = 384
 WIDTH, WINDOW = 288, 208
 NONE = -(1 << 20)
 F32, BF16, I32 = jnp.float32, jnp.bfloat16, jnp.int32
@@ -25,24 +25,58 @@
     return (vf * lax.rsqrt(jnp.mean(vf * vf, axis=-1, keepdims=True) + 1e-6) * g).astype(BF16)
 
 
-def attention(x, wq, wk, wv, wo, g):
-    ns, seq, d = x.shape
-    nh = wq.shape[1] // HEAD
-    xf = x.reshape(ns * seq, d)
-    u = rms(xf, g)
-
-    def proj(w):
-        a = jnp.dot(u, w, preferred_element_type=F32).astype(BF16)
-        return a.reshape(ns, seq, nh, HEAD)
-
-    q, k, v = proj(wq), proj(wk), proj(wv)
-    causal = jnp.arange(seq)[:, None] >= jnp.arange(seq)[None, :]
-    s = jnp.einsum("bqhe,bkhe->bhqk", q, k, preferred_element_type=F32) * HEAD ** -0.5
-    s = jnp.where(causal, s, -1e30)
-    p = jax.nn.softmax(s, axis=-1).astype(BF16)
-    o = jnp.einsum("bhqk,bkhe->bqhe", p, v, preferred_element_type=F32).astype(BF16)
-    a = jnp.dot(o.reshape(ns * seq, nh * HEAD), wo, preferred_element_type=F32)
-    return (xf.astype(F32) + a).astype(BF16)
+def attention_kernel(x, ga, gm, wq, wk, wv, wo, h, z, u, acc):
+    i = pl.program_id(0)
+    t = x.shape[0]
+    half = t // 2
+
+    @pl.when(i == 0)
+    def _():
+        for c in range(4):
+            rows = slice(c * t // 4, (c + 1) * t // 4)
+            u[rows] = rms(x[rows], ga[...])
+        acc[...] = jnp.zeros_like(acc)
+
+    q, k, v = (jnp.dot(u[...], w[...], preferred_element_type=F32).astype(BF16) for w in (wq, wk, wv))
+    heads = []
+    for e in range(q.shape[1] // HEAD):
+        cols = slice(e * HEAD, (e + 1) * HEAD)
+        parts = []
+        for b in range(2):
+            keys = (b + 1) * half
+            w = lax.dot_general(q[b * half:(b + 1) * half, cols], k[:keys, cols], (((1,), (1,)), ((), ())),
+                                preferred_element_type=F32) * HEAD ** -0.5
+            seen = (lax.broadcasted_iota(I32, (half, keys), 0) + b * half) >= lax.broadcasted_iota(I32, (half, keys), 1)
+            w = jnp.where(seen, w, -1e30)
+            p = jnp.exp(w - jnp.max(w, axis=1, keepdims=True))
+            p = (p * (1.0 / jnp.sum(p, axis=1, keepdims=True))).astype(BF16)
+            parts.append(jnp.dot(p, v[:keys, cols], preferred_element_type=F32).astype(BF16))
+        heads.append(jnp.concatenate(parts, 0))
+    acc[...] += jnp.dot(jnp.concatenate(heads, 1), wo[...], preferred_element_type=F32)
+
+    @pl.when(i == pl.num_programs(0) - 1)
+    def _():
+        for c in range(4):
+            rows = slice(c * t // 4, (c + 1) * t // 4)
+            r = (x[rows].astype(F32) + acc[rows]).astype(BF16)
+            h[rows] = r
+            z[rows] = rms(r, gm[...])
+
+
+def attention(x, ga, gm, wq, wk, wv, wo):
+    t, d = x.shape
+    step = 2 * HEAD
+    whole = pl.BlockSpec((t, d), lambda i: (0, 0))
+    gain = pl.BlockSpec((1, d), lambda i: (0, 0))
+    down = pl.BlockSpec((d, step), lambda i: (0, i))
+    out = jax.ShapeDtypeStruct((t, d), BF16)
+    return pl.pallas_call(
+        attention_kernel, grid=(wq.shape[1] // step,), out_shape=[out, out],
+        in_specs=[whole, gain, gain, down, down, down, pl.BlockSpec((step, d), lambda i: (i, 0))],
+        out_specs=[whole, whole], scratch_shapes=[pltpu.VMEM((t, d), BF16), pltpu.VMEM((t, d), F32)],
+        compiler_params=pltpu.CompilerParams(vmem_limit_bytes=67043328), name="attention",
+        cost_estimate=pl.CostEstimate(flops=200_000_000, bytes_accessed=40_000_000, transcendentals=0),
+    )(x, ga[None], gm[None], wq, wk, wv, wo)
 
 
 def capacity(t, top, n_exp):
@@ -66,6 +100,62 @@
 def among(idx, first, n):
     e = first + jnp.arange(n, dtype=I32)
     return idx[:, :, None, :] == e[None, None, :, None]
+
+
+def routes_kernel(top, el, gap, spot, pay, px, pb, gb, tri):
+    nm, ep, _, t = pay.shape
+    nb, _, window = px.shape
+    steps = nb // nm
+    row, chip, core = spot[0], spot[1], spot[2]
+    tri[...] = jnp.where(lax.broadcasted_iota(I32, (t, t), 0) < lax.broadcasted_iota(I32, (t, t), 1), 1.0, 0.0).astype(BF16)
+    per = 2 * el
+    first = (row * 2 + chip) * per
+    e = lax.broadcasted_iota(I32, (per, 1), 0)
+    mine = (first + lax.rem(e + el * core, per)).astype(F32)
+    edge = (row * 2 * per).astype(F32)
+    for n in range(nb):
+        m, r = n // steps, STEPS[n // steps][n % steps]
+
+        def source(i, carry):
+            far_core, far_chip = 1 - i // 2, 1 - lax.rem(i, 2)
+            k = core + far_core - 2 * core * far_core
+            y = chip + far_chip - 2 * chip * far_chip
+            p = lax.rem(row - r + steps, steps) * 4 + y * 2 + k
+            chosen = pay[m, p, 0:top, :]
+            gate = pay[m, p, top:2 * top, :]
+            hit = jnp.zeros((per, t), F32)
+            g = jnp.zeros((per, t), F32)
+            in_a = jnp.zeros((1, t), F32)
+            in_b = jnp.zeros((1, t), F32)
+            for j in range(top):
+                c = chosen[j:j + 1, :]
+                same = c == mine
+                hit = hit + jnp.where(same, 1.0, 0.0)
+                g = g + jnp.where(same, gate[j:j + 1, :], 0.0)
+                in_a = jnp.maximum(in_a, jnp.where((c >= edge) & (c < edge + per), 1.0, 0.0))
+                in_b = jnp.maximum(in_b, jnp.where((c >= edge + per) & (c < edge + 2 * per), 1.0, 0.0))
+            both = in_a * in_b
+            kinds = jnp.concatenate([in_a - both, both, in_b - both, jnp.zeros((5, t), F32)], 0)
+            rank = jnp.dot(jnp.concatenate([hit, kinds], 0).astype(BF16), tri[...], preferred_element_type=F32)
+            na = jnp.sum(in_a - both, axis=1, keepdims=True)
+            place = jnp.where(both > 0, jnp.maximum(na, float(gap)) + rank[per + 1:per + 2],
+                              jnp.where(in_a > 0, rank[per:per + 1],
+                                        jnp.where(in_b > 0, window + gap - 1.0 - rank[per + 2:per + 3], float(NONE))))
+            place = (place - (chip * gap).astype(F32)).astype(I32)
+            one = jnp.where(lax.broadcasted_iota(I32, (window, t), 0) == place, 1.0, 0.0).astype(BF16)
+            wanted = jnp.where(hit > 0, rank[0:per] + 1.0, 0.0).astype(BF16)
+            cols = jnp.concatenate([wanted.astype(F32)] + [v.astype(F32) for v in split3(g)], 0).astype(BF16)
+            rows = lax.dot_general(cols, one, (((1,), (1,)), ((), ())), preferred_element_type=F32)
+            at = rows[0:per].astype(I32) - 1
+            px[n, pl.ds(i * el, el), :] = at[0:el]
+
+            @pl.when(i >= 2)
+            def _():
+                pb[n, pl.ds((i - 2) * per, per), :] = at
+                gb[n, pl.ds((i - 2) * per, per), :] = rows[per:2 * per] + rows[2 * per:3 * per] + rows[3 * per:]
+            return carry
+        for i in range(4):
+            source(i, 0)
 
 
 def list_kernel(pos, z, *outs):
@@ -245,7 +335,7 @@
                 c.wait()
 
             def tile(k, cc):
-                at = pl.ds(pl.multiple_of(e * rows + k * TILE, TILE), TILE)
+                at = pl.ds(pl.multiple_of(e * rows + k * TILE, 32), TILE)
                 for c in range(fb):
                     v = jnp.dot(x[at, :], w13b[s, :, 2 * c * LANES:2 * (c + 1) * LANES], preferred_element_type=F32)
                     act[:, c * LANES:(c + 1) * LANES] = (jax.nn.silu(v[:, :LANES]) * v[:, LANES:]).astype(BF16)
@@ -319,15 +409,24 @@
             go_sum(at[r]).wait_recv()
         refs = [sr.at[at[0]]] + [rr.at[at[r]] for r in range(1, steps)]
         lane = lax.broadcasted_iota(I32, (t, width), 1)
-        run(local(h[m], zin, 0))
+        def pieces(c):
+            return [local(a.at[:, pl.ds(c * quarter, quarter)], ob.at[c % 2, :, pl.ds(l * quarter, quarter)], 4 * (c % 2) + l)
+                    for l, a in enumerate(refs)]
+
+        for w in pieces(0):
+            w.start()
+        run(pltpu.make_async_copy(h[m], zin, psem.at[0, 0]))
         for c in range(4):
             cols = slice(c * quarter, (c + 1) * quarter)
-            spot = lambda l: ob.at[0, :, pl.ds(l * quarter, quarter)]
-            run(*[local(a.at[:, pl.ds(c * quarter, quarter)], spot(l), 1 + l) for l, a in enumerate(refs)])
+            if c + 1 < 4:
+                for w in pieces(c + 1):
+                    w.start()
+            for w in pieces(c):
+                w.wait()
             v = zin[:, cols].astype(F32)
             for r in range(steps):
                 one = jnp.where(lane == homes[m, :, r:r + 1], 1.0, 0.0).astype(BF16)
-                for p in split3(ob[0, :, r * quarter:(r + 1) * quarter]):
+                for p in split3(ob[c % 2, :, r * quarter:(r + 1) * quarter]):
                     v = v + jnp.dot(one, p, preferred_element_type=F32)
             zin[:, cols] = v.astype(BF16)
         run(local(zin, y.at[m], 0))
@@ -412,40 +511,12 @@
             mid = jnp.maximum(na, gap)
             return jnp.where(a & b, mid + only[1], jnp.where(a, only[0], jnp.where(b, width - 1 - only[2], NONE)))
 
-        mine = lax.dynamic_index_in_dim(every, lax.axis_index("dp"), 0, keepdims=False)
-
-        def flip(a, axis, bit):
-            return jnp.where(bit == 0, jnp.flip(a, axis), a)
-
-        def relative(a):
-            a = a.reshape((nrow, 2, 2) + a.shape[1:])
-            a = jnp.flip(lax.dynamic_slice_in_dim(jnp.concatenate([a, a]), row + 1, nrow), 0)
-            return flip(flip(jnp.swapaxes(a, 1, 2), 1, core), 2, chip)
+        mine = lax.dynamic_index_in_dim(jnp.swapaxes(every, 1, 2), lax.axis_index("dp"), 0, keepdims=False)
 
         def lists_of(m, width, window):
             steps = lax.rem(row + jnp.arange(nrow, dtype=I32), nrow)
             own = jnp.broadcast_to(idx[m].reshape(t, top).T[None], (nrow, top, t))
             return places_of(*halves(own, steps[:, None, None]), width - window, width)
-
-        def routes(m, width, window):
-            ia = relative(mine[:, m, :top].astype(I32)).reshape(ep, top, t)
-            ga = relative(mine[:, m, top:2 * top])[:, 1].reshape(ep // 2, top, t)
-            own = lambda a: a.reshape((nrow, 2, 2) + a.shape[1:])[:, 1].reshape((ep // 2,) + a.shape[1:])
-            k = 2 * el
-            hits = among(ia, k * (me // 2), k)
-            pos = ranks(jnp.any(hits, 1))
-            g = jnp.sum(jnp.where(own(hits), ga[:, :, None, :], 0.0), 1)
-            listed = places_of(*halves(ia, row), width - window, width) - chip * (width - window)
-            lists = (listed[:, :, None] == jnp.arange(window, dtype=I32)).astype(BF16)
-            places = jnp.einsum("pet,ptc->pec", (jnp.maximum(pos, -1) + 1).astype(BF16), lists,
-                                preferred_element_type=F32).astype(I32) - 1
-            gs = jnp.einsum("pet,ptc->pec", jnp.concatenate(split3(g), 1), own(lists), preferred_element_type=F32)
-            lgate = gs[:, :k] + gs[:, k:2 * k] + gs[:, 2 * k:]
-            turn = lambda a: jnp.where(core == 0, a, jnp.roll(a, el, axis=1))
-            places = turn(places)
-            lpos = own(places).reshape(nrow, 2 * k, window)
-            lgate = turn(lgate).reshape(nrow, 2 * k, window)
-            return places[:, :el].reshape(nrow, 4 * el, window), lpos, lgate
 
         def layers(width, window, z0, h0, x):
             lists = [lists_of(m, width, window) for m in range(nm)]
@@ -458,13 +529,18 @@
             came = jnp.stack([rows0[r] if r == 0 else lax.ppermute(rows0[r], "row", [(i, (i + r) % nrow) for i in range(nrow)])
                               for r in STEPS[0]])
             x1, _ = lax.optimization_barrier((x[1], rows0[0]))
-            h1 = attention(x1, wq, wk, wv, wo, gattn)
-            z1 = rms(h1, gmoe)
+            h1, z1 = attention(x1.reshape(t, d), gattn, gmoe, wq, wk, wv, wo)
             homes = jnp.stack([jnp.pad(a.T, ((0, 0), (0, LANES - nrow))) for a in lists])
-            rt = [routes(m, width, window) for m in range(nm)]
-            px, pb, gb = (jnp.concatenate([jnp.stack([rt[m][k][r] for r in STEPS[m]]) for m in range(nm)]) for k in range(3))
             nb = nm * nrow
             rows = el * cap
+            table = jax.ShapeDtypeStruct((nb, 4 * el, window), I32)
+            px, pb, gb = pl.pallas_call(
+                functools.partial(routes_kernel, top, el, width - window),
+                out_shape=[table, table, jax.ShapeDtypeStruct(table.shape, F32)],
+                in_specs=[SMEM, VMEM], out_specs=[VMEM] * 3, scratch_shapes=[pltpu.VMEM((t, t), BF16)], name="routes",
+                compiler_params=pltpu.CompilerParams(vmem_limit_bytes=67043328),
+                cost_estimate=pl.CostEstimate(flops=50_000_000, bytes_accessed=2_000_000, transcendentals=0),
+            )(jnp.stack([row, chip, core]).astype(I32), mine)
             wide = jax.ShapeDtypeStruct((nrow, width, d), BF16)
             part = jax.ShapeDtypeStruct((nb, window, d), F32)
             exact = jax.ShapeDtypeStruct((nb, width, d), F32)
@@ -496,8 +572,7 @@
             )(came, z1, h0, h1, lists[1], homes, px, pb, gb, w1, w3, w2)
             return y.reshape(nm, ns, seq, d)
 
-        h0 = attention(x[0], wq, wk, wv, wo, gattn)
-        z0 = rms(h0, gmoe)
+        h0, z0 = attention(x[0].reshape(t, d), gattn, gmoe, wq, wk, wv, wo)
         fits = width_needed(WIDTH - WINDOW) <= WIDTH
         return lax.cond(fits, functools.partial(layers, WIDTH, WINDOW), functools.partial(layers, t, t), z0, h0, x)
 

time: 964 us -> 912 us (0.946)
  matrix products: 109 us -> 5.12 us
  Pallas kernels: 698 us -> 779 us
  other arithmetic: 74.5 us -> 25.3 us
  waiting for transfers between devices: 0.03 us -> 47.2 us
  local copies, waits for them, and re-layouts: 34.3 us -> 21.2 us
  loops' own time: 19.3 us -> 8.07 us
    dot_general x16 -> x0, matrix products: 102 us -> none  [the longest x6 42.3 us: proj(): a = jnp.dot(u, w, preferred_element_type=F32).astype(BF16)]
    pallas_call x0 -> x3, Pallas kernels: none -> 96.3 us  [the longest x2 89.5 us: attention(): pl.pallas_call(attention_kernel, grid=(wq.shape[1] // step,), out_shape=[...]
    sub x2 -> x0, other arithmetic: 35 us -> none  [attention(): p = jax.nn.softmax(s, axis=-1).astype(BF16)]
    ppermute x3, waiting for transfers between devices: 0.01 us -> 34.7 us  [layers(): lax.ppermute(rows0[r], 'row', [(i, (i + r) % nrow) for i in range(nrow)])]
    pallas_call x1, Pallas kernels: 693 us -> 678 us  [layers(): pl.pallas_call(functools.partial(layer_kernel, cap, nrow), out_shape=[jax...]
    all_gather x1, waiting for transfers between devices: 0.01 us -> 12.5 us  [local(): every = lax.all_gather(pay, tok_axes)]
    another operation x1, loops' own time: 19.3 us -> 8.07 us  [local(): lax.cond(fits, functools.partial(layers, WIDTH, WINDOW), functools.partia...]
  transfers between devices with their start and end apart: 4 -> 4, of which waited for: 0 -> 2; matrix products, arithmetic and copies ran while one was open for 19% -> 2% of each run, Pallas kernels for 0% -> 11%
where the time goes in v3:
time: 912 us; the launch traced here: 906 us
  Pallas kernels  779 us (85%)
  waiting for transfers between devices  47.2 us (5%)
  other arithmetic  25.3 us (3%)
  local copies, waits for them, and re-layouts  21.2 us (2%)
  between operations  16.4 us (2%)
    pallas_call x1, Pallas kernels, layers(): pl.pallas_call(functools.partial(layer_kernel, cap, nrow), out_shape=[jax...  678 us
    pallas_call x2, Pallas kernels, attention(): pl.pallas_call(attention_kernel, grid=(wq.shape[1] // step,), out_shape=[...  89.5 us
    ppermute x3, waiting for transfers between devices, layers(): lax.ppermute(rows0[r], 'row', [(i, (i + r) % nrow) for i in range(nrow)])  34.7 us
  transfers between devices with their start and end apart: 4, of which 2 were waited for; matrix products, arithmetic and copies ran while one was open for 2% of the time, Pallas kernels for 11%

profile of v3, /device:TPU:0, one launch (start us, length us, event | category | flops | bytes accessed | tf_op | source)
XLA Modules:
  0.0 906.5 jit_solution(4639469649851700983)
XLA Ops:
  6.5 0.7 copy.309
  7.3 0.7 copy_convert_fusion
  8.1 0.7 maximum_bitcast_fusion
  8.8 3.2 slice_bitcast_fusion.6.x
  12.0 44.7 %attention.5 = (bf16[512,2048]{1,0:T(8,128)(2,1)}, bf16[512,2048]{1,0:T(8,128)(2,1)}) custom-call(bf16[512,2048]{1,0:T(8,128)(2,1)} %slice_bitcast_fusion.6.x, f32[1,2048]{1,0:T(1,128)} %bitcast.267, f32[1,2048]{1,0:T(1,128)} %bitcast.270, bf16[2048,2048]{1,0:T(8,128)(2,1)} %wq.1, bf16[2048,2048]{1,0:T(8,128)(2,1)} %wk.1, bf16[2048,2048]{1,0:T(8,128)(2,1)} %wv.1, ...), custom_call_target="tpu_custom_call" | custom-call | flops 200000000 | bytes 40000000 | tf_op jit(solution)/shard_map/attention/pallas_call | solution.py:73
  56.7 12.5 %all-gather.3.cloned.1.call-done = f32[64,16,512]{2,1,0:T(8,128)} async-done(((f32[2,16,512]{2,1,0:T(8,128)}), f32[64,16,512]{2,1,0:T(8,128)}) %all-gather.3.cloned.1.call-update) | async-done | bytes 2097168 | tf_op jit(solution)/shard_map/all_gather | solution.py:493
  69.2 5.2 compare_reduce_fusion.1
  74.4 2.3 dynamic-slice_bitcast_fusion
  76.7 3.3 fusion.60
  80.6 3.3 fusion.54
  84.2 0.6 add_reduce_fusion.3
  85.7 0.6 add_reduce_fusion.2
  87.0 0.6 add_reduce_fusion.1
  88.3 0.6 add_reduce_fusion
  89.6 804.9 %conditional.1 = (bf16[2,1,512,2048]{3,2,0,1:T(8,128)(2,1)}) conditional(s32[]{:T(128)} %convert_element_type.182, (s32[2,1,512,6]{2,1,3,0:T(1,128)}, s32[]{:T(128)}, bf16[512,2048]{1,0:T(8,128)(2,1)}, bf16[2,1,512,2048]{3,2,1,0:T(8,128)(2,1)}, f32[2048]{0:T(1024)}, /*index=5*/f32[2048]{0:T(1024)}, bf16[2048,2048]{1,0:T(8,128)(2,1)}, ...), branch_computations={%region_24.31_spmd, %region_31.38_spmd} | conditional | flops 327238432 | bytes 112099792 | solution.py:577
  97.3 0.7 copy.324
  98.1 0.7 fusion.41
  98.8 0.2 copy.274
  99.0 0.2 copy.275
  99.2 0.4 convolution_convert_fusion.11
  99.6 1.1 convert_reduce_fusion.3
  100.7 0.1 copy.284
  100.8 0.2 copy.287
  101.0 1.1 select_select_fusion.3
  102.1 0.7 copy.288.pos
  102.8 5.2 lists.3
  108.1 0.4 collective-permute-start.3
  108.5 3.4 collective-permute-start.4
  111.9 0.9 copy.289
  112.8 0.9 copy.290
  113.7 0.4 convolution_convert_fusion.8
  114.1 1.1 convert_reduce_fusion.2
  115.3 0.7 broadcast_select_fusion.2
  115.9 0.1 copy.302
  116.1 3.2 slice_bitcast_fusion.3
  119.3 1.1 select_select_fusion.2
  120.4 0.7 copy.307.lists
  121.1 1.1 copy.355
  122.2 0.6 pad_add_fusion.3.spot
  122.7 6.8 routes.3
  129.5 44.8 %attention.4 = (bf16[512,2048]{1,0:T(8,128)(2,1)}, bf16[512,2048]{1,0:T(8,128)(2,1)}) custom-call(bf16[512,2048]{1,0:T(8,128)(2,1)} %bitcast.256, f32[1,2048]{1,0:T(1,128)} %bitcast.269, f32[1,2048]{1,0:T(1,128)} %bitcast.272, bf16[2048,2048]{1,0:T(8,128)(2,1)} %get-tuple-element.115.wq, bf16[2048,2048]{1,0:T(8,128)(2,1)} %get-tuple-element.116.wk, ...), custom_call_target="tpu_custom_call" | custom-call | flops 200000000 | bytes 40000000 | tf_op jit(solution)/shard_map/cond/branch_1_fun/attention/pallas_call | solution.py:73
  174.3 1.4 fusion.29
  175.8 1.3 fusion.34
  177.1 0.8 pad_add_fusion.2.homes
  178.0 34.7 %collective-permute-done.5 = bf16[288,2048]{1,0:T(8,128)(2,1)} collective-permute-done((bf16[288,2048]{1,0:T(8,128)(2,1)}, bf16[288,2048]{1,0:T(8,128)(2,1)}, u32[]{:S(2)}, u32[]{:S(2)}) %collective-permute-start.5) | collective-permute-done | bytes 1179680 | tf_op jit(solution)/shard_map/cond/branch_1_fun/ppermute | solution.py:529
  212.7 3.8 pad_maximum_fusion.1.z0
  216.5 677.8 %layer.3 = (bf16[2,512,2048]{2,1,0:T(8,128)(2,1)}, bf16[4,288,2048]{2,1,0:T(8,128)(2,1)}, bf16[4,288,2048]{2,1,0:T(8,128)(2,1)}, bf16[8,208,2048]{2,1,0:T(8,128)...) custom-call(bf16[4,288,2048]{2,1,0:T(8,128)(2,1)} %pad_maximum_fusio, ...), custom_call_target="tpu_custom_call" | custom-call | tf_op jit(solution)/shard_map/cond/branch_1_fun/layer/pallas_call | solution.py:548
  894.5 4.8 copy.359
  (48 shorter events, 1.4 us)
Async XLA Ops:
  6.5 62.7 %all-gather.3.cloned.1.call-start = ((), (), s32[]{:S(2)}) async-start(), calls=%async_computation | async-start | bytes 2162688 | tf_op jit(solution)/shard_map/all_gather | solution.py:493
  99.0 2.0 copy-start.5
  99.2 2.9 copy-start.7
  99.6 3.2 copy-start.13
  100.7 2.1 copy-start.17
  108.1 13.0 %copy-start.1 = (f32[1,2,16,16,512]{4,3,1,2,0:T(8,128)S(1)}, f32[1,2,16,16,512]{4,3,1,2,0:T(8,128)}, u32[]{:S(2)}) copy-start(f32[1,2,16,16,512]{4,3,1,2,0:T(8,128)} %get-tuple-element.444) | copy-start | bytes 3145732 | tf_op jit(solution)/shard_map/cond
  108.1 69.9 %collective-permute-start.3 = (bf16[288,2048]{1,0:T(8,128)(2,1)}, bf16[288,2048]{1,0:T(8,128)(2,1)}, u32[]{:S(2)}, u32[]{:S(2)}) collective-permute-start(bf16[288,2048]{1,0:T(8,128)(2,1)} %get-tuple-element.108), channel_id=1, source_target_pairs={{0,4},{4,8},{8,12},{12,0},{1,5},{5,9},{9,13},{13,1},{2,6},{6,10},{... | collective-permute-start | bytes 3538952 | tf_op jit(solution)/shard_map/cond/branch_1_fun/ppermute | solution.py:529
  108.5 69.5 %collective-permute-start.4 = (bf16[288,2048]{1,0:T(8,128)(2,1)}, bf16[288,2048]{1,0:T(8,128)(2,1)}, u32[]{:S(2)}, u32[]{:S(2)}) collective-permute-start(bf16[288,2048]{1,0:T(8,128)(2,1)} %get-tuple-element.109), channel_id=1, source_target_pairs={{0,12},{4,0},{8,4},{12,8},{1,13},{5,1},{9,5},{13,9},{2,14},{6,2},{... | collective-permute-start | bytes 3538952 | tf_op jit(solution)/shard_map/cond/branch_1_fun/ppermute | solution.py:529
  111.9 100.8 %collective-permute-start.5 = (bf16[288,2048]{1,0:T(8,128)(2,1)}, bf16[288,2048]{1,0:T(8,128)(2,1)}, u32[]{:S(2)}, u32[]{:S(2)}) collective-permute-start(bf16[288,2048]{1,0:T(8,128)(2,1)} %get-tuple-element.110), channel_id=1, source_target_pairs={{0,8},{4,12},{8,0},{12,4},{1,9},{5,13},{9,1},{13,5},{2,10},{6,14},... | collective-permute-start | bytes 3538952 | tf_op jit(solution)/shard_map/cond/branch_1_fun/ppermute | solution.py:529
  112.8 9.3 %copy-start.9 = (pred[4,512]{0,1:T(8,128)(4,1)}, pred[4,512]{0,1:T(8,128)(4,1)S(1)}, u32[]{:S(2)}) copy-start(pred[4,512]{0,1:T(8,128)(4,1)S(1)} %copy.289) | copy-start | bytes 6148 | tf_op jit(solution)/shard_map/cond
  113.6 8.5 copy-start.11
  114.0 8.1 copy-start.14
  115.1 7.0 copy-start.19
  174.3 38.3 %copy-start.3 = (bf16[288,2048]{1,0:T(8,128)(2,1)S(1)}, bf16[288,2048]{1,0:T(8,128)(2,1)}, u32[]{:S(2)}) copy-start(bf16[288,2048]{1,0:T(8,128)(2,1)} %get-tuple-element.107) | copy-start | bytes 3538948 | tf_op jit(solution)/shard_map/cond
Sparse Core Ops, SparseCore 0:
  10.2 58.9 all-gather.2

commit v4 on v3

--- a/solution.py
+++ b/solution.py
@@ -65,7 +65,7 @@
 
 def attention(x, ga, gm, wq, wk, wv, wo):
     t, d = x.shape
-    step = 2 * HEAD
+    step = 4 * HEAD
     whole = pl.BlockSpec((t, d), lambda i: (0, 0))
     gain = pl.BlockSpec((1, d), lambda i: (0, 0))
     down = pl.BlockSpec((d, step), lambda i: (0, i))
@@ -168,9 +168,9 @@
             o[:, cols] = jnp.dot(sel, z[:, cols], preferred_element_type=F32).astype(BF16)
 
 
-def layer_kernel(cap, steps, z0, z1, h0, h1, lists, homes, px, pb, gb, w1, w3, w2,
+def layer_kernel(cap, steps, za, zb0, zc, zd, y0, k0, k1, z1, h0, h1, lists, homes, px, pb, gb, w1, w3, w2,
                  y, ls, z2, zy, zk, eo, em, ei, po, pm, pi, sr, rr,
-                 zin, zb, x, act, w13b, w2b, ob, lsem, psem, wsem, send, recv, ksend, krecv):
+                 zin, zb, x, act, w13b, w2b, ob, fa, lsem, psem, fsem, wsem, send, recv, ksend, krecv):
     el, d, f = w1.shape
     t, _ = z1.shape
     h = (h0, h1)
@@ -178,6 +178,10 @@
     nb = steps * nm
     width, window = zb.shape[1], zy.shape[1]
     gap = width - window
+    early = (za, zb0, zc)
+    ne = len(early)
+    turns = fa.shape[1] != width
+    fa = ob if turns else fa
     rows = el * cap
     fb = f // LANES
     quarter = d // 4
@@ -203,36 +207,37 @@
         return pltpu.make_async_remote_copy(src_ref=src, dst_ref=dst, send_sem=send_sem, recv_sem=recv_sem,
                                             device_id=device, device_id_type=MESH)
 
-    def by_half(n, act_on):
+    def arrived(n, act_on):
         if isinstance(n, int):
-            act_on(z0.at[n] if n < steps else z2.at[n - steps])
+            act_on(early[n] if n < ne else z2.at[n - ne])
             return
-
-        @pl.when(n < steps)
-        def _():
-            act_on(z0.at[n])
-
-        @pl.when(n >= steps)
-        def _():
-            act_on(z2.at[n - steps])
+        for j in range(ne):
+            @pl.when(n == j)
+            def _(j=j):
+                act_on(early[j])
+
+        @pl.when(n >= ne)
+        def _():
+            act_on(z2.at[n - ne])
 
     def go_row(n):
-        return pair(ls.at[n - steps], z2.at[n - steps], send.at[0, n], recv.at[0, n], other(step_of(n)))
+        src = z2.at[n - ne] if not isinstance(n, int) else zd if n < steps else ls.at[n - steps]
+        return pair(src, z2.at[n - ne], send.at[0, n], recv.at[0, n], other(step_of(n)))
 
     def go_chip(n, src=None):
-        src = z0.at[0] if src is None else src
+        src = za if src is None else src
         return pair(src.at[far], zy.at[n], send.at[1, n], recv.at[1, n], chip)
 
     def start_chip(n):
-        by_half(n, lambda src: go_chip(n, src).start())
+        arrived(n, lambda src: go_chip(n, src).start())
 
     def go_core(n, i, src=None):
-        src = zy.at[n] if i == 0 else (z0.at[0] if src is None else src).at[near]
+        src = zy.at[n] if i == 0 else (za if src is None else src).at[near]
         return pair(src, zk.at[n, i], ksend.at[n, i], krecv.at[n, i], core)
 
     def start_core(n):
         go_core(n, 0).start()
-        by_half(n, lambda src: go_core(n, 1, src).start())
+        arrived(n, lambda src: go_core(n, 1, src).start())
 
     def go_expert(n):
         return remote(eo, ei, 2, n, core)
@@ -274,11 +279,12 @@
             c.start()
     pl.semaphore_wait(barrier, len(partners))
 
-    start_chip(0)
+    go_row(steps - 1).start()
+    start_chip(1)
     run(local(z1, zin, 0))
     for i, r in enumerate(STEPS[1]):
         n = steps + i
-        put = local(zb.at[i % 2], (z2 if r == 0 else ls).at[i], 1 + i % 2)
+        put = local(zb.at[i % 2], z2.at[n - ne] if r == 0 else ls.at[i], 1 + i % 2)
         sel = jnp.where(hot(lists[r:r + 1, :], width), 1.0, 0.0).astype(BF16)
         for c in range(4):
             cols = slice(c * quarter, (c + 1) * quarter)
@@ -286,10 +292,6 @@
         run(put)
         if r:
             go_row(n).start()
-        if i == 0:
-            go_chip(0).wait_recv()
-            start_core(0)
-            start_chip(1)
 
     def dispatch(n):
         @pl.when(n + 1 < nb)
@@ -299,23 +301,37 @@
 
         @pl.when(n + 2 < nb)
         def _():
-            @pl.when(jnp.logical_and(n + 2 >= steps, step_of(n + 2) != 0))
+            @pl.when(jnp.logical_and(n + 2 >= ne, step_of(n + 2) != 0))
             def _():
                 go_row(n + 2).wait_recv()
             start_chip(n + 2)
 
     def experts(n):
-        for i in range(2):
-            go_core(n, i).wait_recv()
-        srcs = (zk.at[n, 0], zk.at[n, 1], zy.at[n])
-        fetch = lambda i, src: local(src, zb.at[i % 2, pl.ds(0, window)], 1 + i % 2)
-        fetch(0, srcs[0]).start()
+        @pl.when(n > 0)
+        def _():
+            for i in range(2):
+                go_core(n, i).wait_recv()
+
+        def fetch(i, src):
+            return local(src, zb.at[i % 2, pl.ds(0, window)], 1 + i % 2)
+
+        def start(i):
+            if i == 3:
+                arrived(n, lambda src: fetch(3, src.at[near]).start())
+                return
+
+            @pl.when(n == 0)
+            def _():
+                fetch(i, (k0, k1, y0)[i]).start()
+
+            @pl.when(n > 0)
+            def _():
+                fetch(i, (zk.at[n, 0], zk.at[n, 1], zy.at[n])[i]).start()
+        start(0)
         for i in range(4):
-            if i + 1 < 3:
-                fetch(i + 1, srcs[i + 1]).start()
-            elif i + 1 == 3:
-                by_half(n, lambda src: fetch(3, src.at[near]).start())
-            fetch(i, srcs[min(i, 2)]).wait()
+            if i + 1 < 4:
+                start(i + 1)
+            fetch(i, y0).wait()
             sel = jnp.concatenate([jnp.where(hot(px[n, i * el + e:i * el + e + 1, :], cap), 1.0, 0.0).astype(BF16)
                                    for e in range(el)], 0)
             for c in range(4):
@@ -323,6 +339,11 @@
                 v = jnp.dot(sel, zb[i % 2, 0:window, cols], preferred_element_type=F32).astype(BF16)
                 for e in range(el):
                     x[e * rows + i * cap:e * rows + (i + 1) * cap, cols] = v[e * cap:(e + 1) * cap]
+
+        if not turns:
+            @pl.when(n >= 3)
+            def _():
+                send_on(n - 3)
 
         def put(e, i):
             return pltpu.make_async_copy(x.at[pl.ds(pl.multiple_of(e * rows + i * cap, 32), cap)],
@@ -385,19 +406,29 @@
             else:
                 put.wait()
 
-    def forward(n):
+    def adding(n):
+        return (pltpu.make_async_copy(pm.at[n], fa.at[0, near], fsem.at[0]),
+                pltpu.make_async_copy(pi.at[n], fa.at[1, far], fsem.at[1]))
+
+    def summed(n):
+        return pltpu.make_async_copy(fa.at[0], sr.at[n], fsem.at[2])
+
+    def add_start(n):
         go_part(n).wait_recv()
-
-        copies = (local(pm.at[n], ob.at[0, near], 1), local(pi.at[n], ob.at[1, far], 2))
-        for c in copies:
+        for c in adding(n):
             c.start()
+
+    def add_end(n):
         if gap:
             for i, first in enumerate((1 - col // 2, col // 2)):
-                ob[i, pl.ds(pl.multiple_of(window * first, 16), gap), :] = jnp.zeros((gap, d), F32)
-        for c in copies:
+                fa[i, pl.ds(pl.multiple_of(window * first, 16), gap), :] = jnp.zeros((gap, d), F32)
+        for c in adding(n):
             c.wait()
-        ob[0] = ob[0] + ob[1]
-        run(local(ob.at[0], sr.at[n], 1))
+        fa[0] = fa[0] + fa[1]
+        summed(n).start()
+
+    def send_on(n):
+        summed(n).wait()
 
         @pl.when(step_of(n) != 0)
         def _():
@@ -437,13 +468,26 @@
             dispatch(n)
             experts(n)
 
+        if not turns:
+            @pl.when(n >= nb)
+            def _():
+                send_on(n - 3)
+
+            @pl.when(jnp.logical_and(n >= 2, n <= nb + 1))
+            def _():
+                add_start(n - 2)
+
         @pl.when(jnp.logical_and(n >= 1, n <= nb))
         def _():
             combine(n - 1)
 
         @pl.when(jnp.logical_and(n >= 2, n <= nb + 1))
         def _():
-            forward(n - 2)
+            if turns:
+                add_start(n - 2)
+            add_end(n - 2)
+            if turns:
+                send_on(n - 2)
 
         @pl.when(n == nb - 1)
         def _():
@@ -456,14 +500,19 @@
     lax.fori_loop(0, nb + 3, block, 0)
 
     def drain(n, carry):
-        for c in (go_chip(n), go_core(n, 0), go_core(n, 1), go_expert(n), go_part(n)):
+        for c in (go_expert(n), go_part(n)):
             c.wait_send()
 
+        @pl.when(n > 0)
+        def _():
+            for c in (go_chip(n), go_core(n, 0), go_core(n, 1)):
+                c.wait_send()
+
         @pl.when(step_of(n) != 0)
         def _():
             go_sum(n).wait_send()
 
-            @pl.when(n >= steps)
+            @pl.when(n >= ne)
             def _():
                 go_row(n).wait_send()
         return carry
@@ -526,8 +575,12 @@
                 compiler_params=pltpu.CompilerParams(vmem_limit_bytes=67043328),
                 cost_estimate=pl.CostEstimate(flops=50_000_000, bytes_accessed=7_000_000, transcendentals=0),
             )(lists[0], z0)
-            came = jnp.stack([rows0[r] if r == 0 else lax.ppermute(rows0[r], "row", [(i, (i + r) % nrow) for i in range(nrow)])
-                              for r in STEPS[0]])
+            gap = width - window
+            came = [rows0[r] if r == 0 else lax.ppermute(rows0[r], "row", [(i, (i + r) % nrow) for i in range(nrow)])
+                    for r in STEPS[0][:3]]
+            part_of = lambda c: lax.dynamic_slice_in_dim(rows0[0], gap * c, window)
+            y0 = lax.ppermute(part_of(1 - chip), "col", [(i, (i + 2) % ncol) for i in range(ncol)])
+            k0, k1 = (lax.ppermute(a, "col", [(i, i + 1 - 2 * (i % 2)) for i in range(ncol)]) for a in (y0, part_of(chip)))
             x1, _ = lax.optimization_barrier((x[1], rows0[0]))
             h1, z1 = attention(x1.reshape(t, d), gattn, gmoe, wq, wk, wv, wo)
             homes = jnp.stack([jnp.pad(a.T, ((0, 0), (0, LANES - nrow))) for a in lists])
@@ -542,14 +595,15 @@
                 cost_estimate=pl.CostEstimate(flops=50_000_000, bytes_accessed=2_000_000, transcendentals=0),
             )(jnp.stack([row, chip, core]).astype(I32), mine)
             wide = jax.ShapeDtypeStruct((nrow, width, d), BF16)
+            late = jax.ShapeDtypeStruct((nb - 3, width, d), BF16)
             part = jax.ShapeDtypeStruct((nb, window, d), F32)
             exact = jax.ShapeDtypeStruct((nb, width, d), F32)
             pair = jax.ShapeDtypeStruct((nb, 2, rows, d), BF16)
             y, *_ = pl.pallas_call(
                 functools.partial(layer_kernel, cap, nrow),
-                out_shape=[jax.ShapeDtypeStruct((nm, t, d), BF16), wide, wide, jax.ShapeDtypeStruct((nb, window, d), BF16),
+                out_shape=[jax.ShapeDtypeStruct((nm, t, d), BF16), wide, late, jax.ShapeDtypeStruct((nb, window, d), BF16),
                            jax.ShapeDtypeStruct((nb, 2, window, d), BF16), pair, pair, pair] + [part] * 3 + [exact] * 2,
-                in_specs=[ANY] * 4 + [VMEM] * 5 + [ANY] * 3, out_specs=[ANY] * 13,
+                in_specs=[ANY] * 10 + [VMEM] * 5 + [ANY] * 3, out_specs=[ANY] * 13,
                 scratch_shapes=[
                     pltpu.VMEM((t, d), BF16),
                     pltpu.VMEM((2, width, d), BF16),
@@ -558,8 +612,10 @@
                     pltpu.VMEM((2, d, 2 * f), BF16),
                     pltpu.VMEM((2, f, d), BF16),
                     pltpu.VMEM((2, width, d), F32),
+                    pltpu.VMEM((2, width if window < width else 16, d), F32),
                     pltpu.SemaphoreType.DMA((8,)),
                     pltpu.SemaphoreType.DMA((el, 4)),
+                    pltpu.SemaphoreType.DMA((3,)),
                     pltpu.SemaphoreType.DMA((2, 2 * (f // LANES) + 1)),
                     pltpu.SemaphoreType.DMA((5, nb)),
                     pltpu.SemaphoreType.DMA((5, nb)),
@@ -569,7 +625,7 @@
                 compiler_params=pltpu.CompilerParams(vmem_limit_bytes=67043328, has_side_effects=True,
                                                      collective_id=0 if width < t else 1),
                 name="layer",
-            )(came, z1, h0, h1, lists[1], homes, px, pb, gb, w1, w3, w2)
+            )(*came, rows0[STEPS[0][3]], y0, k0, k1, z1, h0, h1, lists[1], homes, px, pb, gb, w1, w3, w2)
             return y.reshape(nm, ns, seq, d)
 
         h0, z0 = attention(x[0].reshape(t, d), gattn, gmoe, wq, wk, wv, wo)

time: 912 us -> 910 us (level)
  the two profiles are of different devices: /device:TPU:0 before, /device:TPU:28 now
where the time goes in v4:
time: 910 us; the launch traced here: 903 us
  Pallas kernels  812 us (89%)
  local copies, waits for them, and re-layouts  23.3 us (3%)
  other arithmetic  20.8 us (2%)
  between operations  16.5 us (2%)
  waiting for transfers between devices  14.1 us (2%)
    pallas_call x1, Pallas kernels, layers(): pl.pallas_call(functools.partial(layer_kernel, cap, nrow), out_shape=[jax...  720 us
    pallas_call x2, Pallas kernels, attention(): pl.pallas_call(attention_kernel, grid=(wq.shape[1] // step,), out_shape=[...  80.6 us
  transfers between devices with their start and end apart: 6, of which 1 were waited for; matrix products, arithmetic and copies ran while one was open for 2% of the time, Pallas kernels for 10%

profile of v4, /device:TPU:28, one launch (start us, length us, event | category | flops | bytes accessed | tf_op | source)
XLA Modules:
  0.0 903.0 jit_solution(8419788933189545798)
XLA Ops:
  6.5 0.7 copy.303
  7.3 0.7 copy_convert_fusion
  8.1 0.7 maximum_bitcast_fusion
  8.8 3.2 slice_bitcast_fusion.6.x
  12.0 40.2 %attention.5 = (bf16[512,2048]{1,0:T(8,128)(2,1)}, bf16[512,2048]{1,0:T(8,128)(2,1)}) custom-call(bf16[512,2048]{1,0:T(8,128)(2,1)} %slice_bitcast_fusion.6.x, f32[1,2048]{1,0:T(1,128)} %bitcast.251, f32[1,2048]{1,0:T(1,128)} %bitcast.254, bf16[2048,2048]{1,0:T(8,128)(2,1)} %wq.1, bf16[2048,2048]{1,0:T(8,128)(2,1)} %wk.1, bf16[2048,2048]{1,0:T(8,128)(2,1)} %wv.1, ...), custom_call_target="tpu_custom_call" | custom-call | flops 200000000 | bytes 40000000 | tf_op jit(solution)/shard_map/attention/pallas_call | solution.py:73
  52.2 14.0 %all-gather.3.cloned.1.call-done = f32[64,16,512]{2,1,0:T(8,128)} async-done(((f32[2,16,512]{2,1,0:T(8,128)}), f32[64,16,512]{2,1,0:T(8,128)}) %all-gather.3.cloned.1.call-update) | async-done | bytes 2097168 | tf_op jit(solution)/shard_map/all_gather | solution.py:542
  66.3 5.2 compare_reduce_fusion.1
  71.5 2.3 dynamic-slice_bitcast_fusion
  73.8 3.3 fusion.60
  77.6 3.3 fusion.54
  81.2 0.6 add_reduce_fusion.3
  82.8 0.6 add_reduce_fusion.2
  84.1 0.6 add_reduce_fusion.1
  85.4 0.6 add_reduce_fusion
  86.7 804.3 %conditional.1 = (bf16[2,1,512,2048]{3,2,0,1:T(8,128)(2,1)}) conditional(s32[]{:T(128)} %convert_element_type.182, (s32[2,1,512,6]{2,1,3,0:T(1,128)S(1)}, s32[]{:T(128)}, bf16[512,2048]{1,0:T(8,128)(2,1)}, bf16[2,1,512,2048]{3,2,1,0:T(8,128)(2,1)}, f32[2048]{0:T(1024)}, /*index=5*/f32[2048]{0:T(1024)}, bf16[2048,2048]{1,0:T(8,128)(2,1)}, ...), branch_computations={%region_24.31_spmd, %region_31.38_spmd} | conditional | flops 314655520 | bytes 103711136 | solution.py:633
  94.6 0.7 fusion.41
  95.3 0.2 copy.268
  95.5 0.2 copy.269
  95.7 0.4 convolution_convert_fusion.11
  96.1 1.1 convert_reduce_fusion.3
  97.3 0.1 copy.278
  97.4 0.2 copy.281
  97.6 1.1 select_select_fusion.3
  98.7 0.7 copy.282.pos
  99.4 5.2 lists.3
  104.6 1.6 collective-permute-start.5
  106.2 0.4 collective-permute-start.6
  106.6 2.8 constant_dynamic-slice_fusion
  109.5 0.5 collective-permute-start.7
  110.0 0.9 copy.283
  110.9 0.9 copy.284
  111.8 0.4 convolution_convert_fusion.8
  112.2 1.1 convert_reduce_fusion.2
  113.3 0.1 copy.293
  113.4 0.1 copy.296
  113.5 3.2 slice_bitcast_fusion.3
  116.7 1.1 select_select_fusion.2
  117.8 0.7 copy.301.lists
  118.5 1.1 copy.319.pay
  119.6 0.7 pad_add_fusion.3.spot
  120.2 6.8 routes.3
  127.0 40.4 %attention.4 = (bf16[512,2048]{1,0:T(8,128)(2,1)}, bf16[512,2048]{1,0:T(8,128)(2,1)}) custom-call(bf16[512,2048]{1,0:T(8,128)(2,1)} %bitcast.244, f32[1,2048]{1,0:T(1,128)} %bitcast.253, f32[1,2048]{1,0:T(1,128)} %bitcast.256, bf16[2048,2048]{1,0:T(8,128)(2,1)} %get-tuple-element.116.wq, bf16[2048,2048]{1,0:T(8,128)(2,1)} %get-tuple-element.117.wk, ...), custom_call_target="tpu_custom_call" | custom-call | flops 200000000 | bytes 40000000 | tf_op jit(solution)/shard_map/cond/branch_1_fun/attention/pallas_call | solution.py:73
  167.4 0.3 collective-permute-start.8
  167.7 1.3 fusion.29
  169.0 1.3 fusion.34
  170.4 0.8 pad_add_fusion.2.homes
  171.2 719.5 %layer.3 = (bf16[2,512,2048]{2,1,0:T(8,128)(2,1)}, bf16[4,288,2048]{2,1,0:T(8,128)(2,1)}, bf16[5,288,2048]{2,1,0:T(8,128)(2,1)}, bf16[8,208,2048]{2,1,0:T(8,128)...) custom-call(bf16[288,2048]{1,0:T(8,128)(2,1)} %get-tuple-element.107, ...), custom_call_target="tpu_custom_call" | custom-call | tf_op jit(solution)/shard_map/cond/branch_1_fun/layer/pallas_call | solution.py:602
  891.0 4.8 copy.349
  (54 shorter events, 1.3 us)
Async XLA Ops:
  6.5 59.7 %all-gather.3.cloned.1.call-start = ((), (), s32[]{:S(2)}) async-start(), calls=%async_computation | async-start | bytes 2162688 | tf_op jit(solution)/shard_map/all_gather | solution.py:542
  52.2 34.5 %copy-start.14 = (s32[2,1,512,6]{2,1,3,0:T(1,128)S(1)}, s32[2,1,512,6]{2,1,3,0:T(1,128)}, u32[]{:S(2)}) copy-start(s32[2,1,512,6]{2,1,3,0:T(1,128)} %param.15) | copy-start | bytes 73732
  95.5 2.0 copy-start.2
  95.7 2.9 copy-start.3
  96.1 3.2 copy-start.10
  97.3 2.1 copy-start.16
  104.6 8.8 copy-start.15
  104.6 66.6 %collective-permute-start.5 = (bf16[288,2048]{1,0:T(8,128)(2,1)}, bf16[288,2048]{1,0:T(8,128)(2,1)}, u32[]{:S(2)}, u32[]{:S(2)}) collective-permute-start(bf16[288,2048]{1,0:T(8,128)(2,1)} %get-tuple-element.108), channel_id=1, source_target_pairs={{0,4},{4,8},{8,12},{12,0},{1,5},{5,9},{9,13},{13,1},{2,6},{6,10},{... | collective-permute-start | bytes 3538952 | tf_op jit(solution)/shard_map/cond/branch_1_fun/ppermute | solution.py:579
  106.2 65.0 %collective-permute-start.6 = (bf16[288,2048]{1,0:T(8,128)(2,1)}, bf16[288,2048]{1,0:T(8,128)(2,1)}, u32[]{:S(2)}, u32[]{:S(2)}) collective-permute-start(bf16[288,2048]{1,0:T(8,128)(2,1)} %get-tuple-element.109), channel_id=1, source_target_pairs={{0,12},{4,0},{8,4},{12,8},{1,13},{5,1},{9,5},{13,9},{2,14},{6,2},{... | collective-permute-start | bytes 3538952 | tf_op jit(solution)/shard_map/cond/branch_1_fun/ppermute | solution.py:579
  109.5 61.8 %collective-permute-start.9 = (bf16[208,2048]{1,0:T(8,128)(2,1)}, bf16[208,2048]{1,0:T(8,128)(2,1)}, u32[]{:S(2)}, u32[]{:S(2)}) collective-permute-start(bf16[208,2048]{1,0:T(8,128)(2,1)} %get-tuple-element.371), channel_id=1, source_target_pairs={{0,1},{1,0},{2,3},{3,2},{4,5},{5,4},{6,7},{7,6},{8,9},{9,8},{10,11... | collective-permute-start | bytes 2555912 | tf_op jit(solution)/shard_map/cond/branch_1_fun/ppermute | solution.py:583
  109.5 58.0 %collective-permute-start.7 = (bf16[208,2048]{1,0:T(8,128)(2,1)}, bf16[208,2048]{1,0:T(8,128)(2,1)}, u32[]{:S(2)}, u32[]{:S(2)}) collective-permute-start(bf16[208,2048]{1,0:T(8,128)(2,1)} %get-tuple-element.372), channel_id=1, source_target_pairs={{0,2},{1,3},{2,0},{3,1},{4,6},{5,7},{6,4},{7,5},{8,10},{9,11},{10,... | collective-permute-start | bytes 2555912 | tf_op jit(solution)/shard_map/cond/branch_1_fun/ppermute | solution.py:582
  110.9 6.9 copy-start.6
  111.7 6.0 copy-start.8
  111.8 6.8 copy-start.1
  112.2 7.4 copy-start.12
  113.3 6.3 copy-start.18
  167.4 3.8 collective-permute-start.8
Sparse Core Ops, SparseCore 0:
  10.2 56.0 all-gather.2

commit v5 on v3

--- a/solution.py
+++ b/solution.py
@@ -17,7 +17,7 @@
 SMEM = pl.BlockSpec(memory_space=pltpu.SMEM)
 VMEM = pl.BlockSpec(memory_space=pltpu.VMEM)
 MESH = pl.DeviceIdType.MESH
-STEPS = ((0, 1, 3, 2), (2, 3, 1, 0))
+STEPS = ((1, 3, 2, 0), (2, 3, 1, 0))
 
 
 def rms(v, g):
@@ -65,7 +65,7 @@
 
 def attention(x, ga, gm, wq, wk, wv, wo):
     t, d = x.shape
-    step = 2 * HEAD
+    step = 4 * HEAD
     whole = pl.BlockSpec((t, d), lambda i: (0, 0))
     gain = pl.BlockSpec((1, d), lambda i: (0, 0))
     down = pl.BlockSpec((d, step), lambda i: (0, i))
@@ -168,9 +168,9 @@
             o[:, cols] = jnp.dot(sel, z[:, cols], preferred_element_type=F32).astype(BF16)
 
 
-def layer_kernel(cap, steps, z0, z1, h0, h1, lists, homes, px, pb, gb, w1, w3, w2,
+def layer_kernel(cap, steps, za, zb0, zc, zd, z1, h0, h1, lists, homes, px, pb, gb, w1, w3, w2,
                  y, ls, z2, zy, zk, eo, em, ei, po, pm, pi, sr, rr,
-                 zin, zb, x, act, w13b, w2b, ob, lsem, psem, wsem, send, recv, ksend, krecv):
+                 zin, zb, x, act, w13b, w2b, ob, lsem, psem, fsem, wsem, send, recv, ksend, krecv):
     el, d, f = w1.shape
     t, _ = z1.shape
     h = (h0, h1)
@@ -178,6 +178,7 @@
     nb = steps * nm
     width, window = zb.shape[1], zy.shape[1]
     gap = width - window
+    early = {0: za, 1: zb0, 3: zc}
     rows = el * cap
     fb = f // LANES
     quarter = d // 4
@@ -192,7 +193,8 @@
 
     def step_of(n):
         i = lax.rem(n, steps)
-        i = i + (n // steps) * (steps - 1 - 2 * i)
+        k = lax.rem(i + 1, steps)
+        i = k + (n // steps) * (steps - 1 - i - k)
         return lax.rem(i * (i + 1) // 2, steps)
 
     def remote(src, dst, kind, n, device):
@@ -203,36 +205,40 @@
         return pltpu.make_async_remote_copy(src_ref=src, dst_ref=dst, send_sem=send_sem, recv_sem=recv_sem,
                                             device_id=device, device_id_type=MESH)
 
-    def by_half(n, act_on):
+    def arrived(n, act_on):
         if isinstance(n, int):
-            act_on(z0.at[n] if n < steps else z2.at[n - steps])
+            act_on(early.get(n, z2.at[n]))
             return
-
-        @pl.when(n < steps)
-        def _():
-            act_on(z0.at[n])
-
-        @pl.when(n >= steps)
-        def _():
-            act_on(z2.at[n - steps])
+        late = n >= 0
+        for j, ref in early.items():
+            late = jnp.logical_and(late, n != j)
+
+            @pl.when(n == j)
+            def _(ref=ref):
+                act_on(ref)
+
+        @pl.when(late)
+        def _():
+            act_on(z2.at[n])
 
     def go_row(n):
-        return pair(ls.at[n - steps], z2.at[n - steps], send.at[0, n], recv.at[0, n], other(step_of(n)))
+        src = z2.at[n] if not isinstance(n, int) else zd if n < steps else ls.at[n]
+        return pair(src, z2.at[n], send.at[0, n], recv.at[0, n], other(step_of(n)))
 
     def go_chip(n, src=None):
-        src = z0.at[0] if src is None else src
+        src = za if src is None else src
         return pair(src.at[far], zy.at[n], send.at[1, n], recv.at[1, n], chip)
 
     def start_chip(n):
-        by_half(n, lambda src: go_chip(n, src).start())
+        arrived(n, lambda src: go_chip(n, src).start())
 
     def go_core(n, i, src=None):
-        src = zy.at[n] if i == 0 else (z0.at[0] if src is None else src).at[near]
+        src = zy.at[n] if i == 0 else (za if src is None else src).at[near]
         return pair(src, zk.at[n, i], ksend.at[n, i], krecv.at[n, i], core)
 
     def start_core(n):
         go_core(n, 0).start()
-        by_half(n, lambda src: go_core(n, 1, src).start())
+        arrived(n, lambda src: go_core(n, 1, src).start())
 
     def go_expert(n):
         return remote(eo, ei, 2, n, core)
@@ -275,10 +281,12 @@
     pl.semaphore_wait(barrier, len(partners))
 
     start_chip(0)
+    start_chip(1)
+    go_row(2).start()
     run(local(z1, zin, 0))
     for i, r in enumerate(STEPS[1]):
         n = steps + i
-        put = local(zb.at[i % 2], (z2 if r == 0 else ls).at[i], 1 + i % 2)
+        put = local(zb.at[i % 2], (z2 if r == 0 else ls).at[n], 1 + i % 2)
         sel = jnp.where(hot(lists[r:r + 1, :], width), 1.0, 0.0).astype(BF16)
         for c in range(4):
             cols = slice(c * quarter, (c + 1) * quarter)
@@ -286,10 +294,8 @@
         run(put)
         if r:
             go_row(n).start()
-        if i == 0:
-            go_chip(0).wait_recv()
-            start_core(0)
-            start_chip(1)
+    go_chip(0).wait_recv()
+    start_core(0)
 
     def dispatch(n):
         @pl.when(n + 1 < nb)
@@ -299,7 +305,7 @@
 
         @pl.when(n + 2 < nb)
         def _():
-            @pl.when(jnp.logical_and(n + 2 >= steps, step_of(n + 2) != 0))
+            @pl.when(step_of(n + 2) != 0)
             def _():
                 go_row(n + 2).wait_recv()
             start_chip(n + 2)
@@ -307,15 +313,20 @@
     def experts(n):
         for i in range(2):
             go_core(n, i).wait_recv()
-        srcs = (zk.at[n, 0], zk.at[n, 1], zy.at[n])
-        fetch = lambda i, src: local(src, zb.at[i % 2, pl.ds(0, window)], 1 + i % 2)
-        fetch(0, srcs[0]).start()
+
+        def fetch(i, src):
+            return local(src, zb.at[i % 2, pl.ds(0, window)], 1 + i % 2)
+
+        def start(i):
+            if i == 3:
+                arrived(n, lambda src: fetch(3, src.at[near]).start())
+            else:
+                fetch(i, (zk.at[n, 0], zk.at[n, 1], zy.at[n])[i]).start()
+        start(0)
         for i in range(4):
-            if i + 1 < 3:
-                fetch(i + 1, srcs[i + 1]).start()
-            elif i + 1 == 3:
-                by_half(n, lambda src: fetch(3, src.at[near]).start())
-            fetch(i, srcs[min(i, 2)]).wait()
+            if i + 1 < 4:
+                start(i + 1)
+            fetch(i, zy.at[n]).wait()
             sel = jnp.concatenate([jnp.where(hot(px[n, i * el + e:i * el + e + 1, :], cap), 1.0, 0.0).astype(BF16)
                                    for e in range(el)], 0)
             for c in range(4):
@@ -353,13 +364,17 @@
                     c.start()
             return carry
         lax.fori_loop(0, el, expert, 0)
+        dispatch(n)
+
+        @pl.when(n >= 1)
+        def _():
+            add_start(n - 1)
         for e in range(el):
             for i in range(4):
                 put(e, i).wait()
         go_expert(n).start()
 
     def combine(n):
-        go_expert(n).wait_recv()
         fetch = lambda i: (local(em.at[n, i], x.at[pl.ds(2 * i * rows, rows)], 1 + 2 * i),
                            local(ei.at[n, i], x.at[pl.ds((2 * i + 1) * rows, rows)], 2 + 2 * i))
         for i in range(2):
@@ -385,19 +400,29 @@
             else:
                 put.wait()
 
-    def forward(n):
+    def adding(n):
+        return (pltpu.make_async_copy(pm.at[n], ob.at[0, near], fsem.at[0]),
+                pltpu.make_async_copy(pi.at[n], ob.at[1, far], fsem.at[1]))
+
+    def summed(n):
+        return pltpu.make_async_copy(ob.at[0], sr.at[n], fsem.at[2])
+
+    def add_start(n):
         go_part(n).wait_recv()
-
-        copies = (local(pm.at[n], ob.at[0, near], 1), local(pi.at[n], ob.at[1, far], 2))
-        for c in copies:
+        for c in adding(n):
             c.start()
+
+    def add_end(n):
         if gap:
             for i, first in enumerate((1 - col // 2, col // 2)):
                 ob[i, pl.ds(pl.multiple_of(window * first, 16), gap), :] = jnp.zeros((gap, d), F32)
-        for c in copies:
+        for c in adding(n):
             c.wait()
         ob[0] = ob[0] + ob[1]
-        run(local(ob.at[0], sr.at[n], 1))
+        summed(n).start()
+
+    def send_on(n):
+        summed(n).wait()
 
         @pl.when(step_of(n) != 0)
         def _():
@@ -434,26 +459,37 @@
     def block(n, carry):
         @pl.when(n < nb)
         def _():
-            dispatch(n)
             experts(n)
 
-        @pl.when(jnp.logical_and(n >= 1, n <= nb))
-        def _():
-            combine(n - 1)
-
-        @pl.when(jnp.logical_and(n >= 2, n <= nb + 1))
-        def _():
-            forward(n - 2)
-
-        @pl.when(n == nb - 1)
+        @pl.when(n == nb)
+        def _():
+            add_start(n - 1)
+
+        @pl.when(n >= 1)
+        def _():
+            add_end(n - 1)
+
+        @pl.when(n < nb)
+        def _():
+            go_expert(n).wait_recv()
+
+        @pl.when(n >= 1)
+        def _():
+            send_on(n - 1)
+
+        @pl.when(n < nb)
+        def _():
+            combine(n)
+
+        @pl.when(n == nb - 2)
         def _():
             finish(0)
 
-        @pl.when(n == nb + 2)
+        @pl.when(n == nb)
         def _():
             finish(1)
         return carry
-    lax.fori_loop(0, nb + 3, block, 0)
+    lax.fori_loop(0, nb + 1, block, 0)
 
     def drain(n, carry):
         for c in (go_chip(n), go_core(n, 0), go_core(n, 1), go_expert(n), go_part(n)):
@@ -463,7 +499,7 @@
         def _():
             go_sum(n).wait_send()
 
-            @pl.when(n >= steps)
+            @pl.when(n >= 2)
             def _():
                 go_row(n).wait_send()
         return carry
@@ -526,8 +562,7 @@
                 compiler_params=pltpu.CompilerParams(vmem_limit_bytes=67043328),
                 cost_estimate=pl.CostEstimate(flops=50_000_000, bytes_accessed=7_000_000, transcendentals=0),
             )(lists[0], z0)
-            came = jnp.stack([rows0[r] if r == 0 else lax.ppermute(rows0[r], "row", [(i, (i + r) % nrow) for i in range(nrow)])
-                              for r in STEPS[0]])
+            came = [lax.ppermute(rows0[r], "row", [(i, (i + r) % nrow) for i in range(nrow)]) for r in STEPS[0][:2]]
             x1, _ = lax.optimization_barrier((x[1], rows0[0]))
             h1, z1 = attention(x1.reshape(t, d), gattn, gmoe, wq, wk, wv, wo)
             homes = jnp.stack([jnp.pad(a.T, ((0, 0), (0, LANES - nrow))) for a in lists])
@@ -541,7 +576,7 @@
                 compiler_params=pltpu.CompilerParams(vmem_limit_bytes=67043328),
                 cost_estimate=pl.CostEstimate(flops=50_000_000, bytes_accessed=2_000_000, transcendentals=0),
             )(jnp.stack([row, chip, core]).astype(I32), mine)
-            wide = jax.ShapeDtypeStruct((nrow, width, d), BF16)
+            wide = jax.ShapeDtypeStruct((nb, width, d), BF16)
             part = jax.ShapeDtypeStruct((nb, window, d), F32)
             exact = jax.ShapeDtypeStruct((nb, width, d), F32)
             pair = jax.ShapeDtypeStruct((nb, 2, rows, d), BF16)
@@ -549,7 +584,7 @@
                 functools.partial(layer_kernel, cap, nrow),
                 out_shape=[jax.ShapeDtypeStruct((nm, t, d), BF16), wide, wide, jax.ShapeDtypeStruct((nb, window, d), BF16),
                            jax.ShapeDtypeStruct((nb, 2, window, d), BF16), pair, pair, pair] + [part] * 3 + [exact] * 2,
-                in_specs=[ANY] * 4 + [VMEM] * 5 + [ANY] * 3, out_specs=[ANY] * 13,
+                in_specs=[ANY] * 7 + [VMEM] * 5 + [ANY] * 3, out_specs=[ANY] * 13,
                 scratch_shapes=[
                     pltpu.VMEM((t, d), BF16),
                     pltpu.VMEM((2, width, d), BF16),
@@ -560,6 +595,7 @@
                     pltpu.VMEM((2, width, d), F32),
                     pltpu.SemaphoreType.DMA((8,)),
                     pltpu.SemaphoreType.DMA((el, 4)),
+                    pltpu.SemaphoreType.DMA((3,)),
                     pltpu.SemaphoreType.DMA((2, 2 * (f // LANES) + 1)),
                     pltpu.SemaphoreType.DMA((5, nb)),
                     pltpu.SemaphoreType.DMA((5, nb)),
@@ -569,7 +605,7 @@
                 compiler_params=pltpu.CompilerParams(vmem_limit_bytes=67043328, has_side_effects=True,
                                                      collective_id=0 if width < t else 1),
                 name="layer",
-            )(came, z1, h0, h1, lists[1], homes, px, pb, gb, w1, w3, w2)
+            )(*came, rows0[0], rows0[STEPS[0][2]], z1, h0, h1, lists[1], homes, px, pb, gb, w1, w3, w2)
             return y.reshape(nm, ns, seq, d)
 
         h0, z0 = attention(x[0].reshape(t, d), gattn, gmoe, wq, wk, wv, wo)

time: 912 us -> 790 us (0.87)
  Pallas kernels: 779 us -> 691 us
  waiting for transfers between devices: 47.2 us -> 17 us
    pallas_call x1, Pallas kernels: 678 us -> 598 us  [layers(): pl.pallas_call(functools.partial(layer_kernel, cap, nrow), out_shape=[jax...]
    ppermute x3 -> x2, waiting for transfers between devices: 34.7 us -> 0.01 us  [layers(): lax.ppermute(rows0[r], 'row', [(i, (i + r) % nrow) for i in range(nrow)])]
  transfers between devices with their start and end apart: 4 -> 3, of which waited for: 2 -> 1; matrix products, arithmetic and copies ran while one was open for 2% -> 2% of each run, Pallas kernels for 11% -> 11%
where the time goes in v5:
time: 790 us; the launch traced here: 783 us
  Pallas kernels  691 us (87%)
  other arithmetic  21.5 us (3%)
  local copies, waits for them, and re-layouts  20.5 us (3%)
  waiting for transfers between devices  17 us (2%)
  between operations  16.4 us (2%)
  loops' own time  8.05 us (1%)
    pallas_call x1, Pallas kernels, layers(): pl.pallas_call(functools.partial(layer_kernel, cap, nrow), out_shape=[jax...  598 us
    pallas_call x2, Pallas kernels, attention(): pl.pallas_call(attention_kernel, grid=(wq.shape[1] // step,), out_shape=[...  80.5 us
    all_gather x1, waiting for transfers between devices, local(): every = lax.all_gather(pay, tok_axes)  17 us
  transfers between devices with their start and end apart: 3, of which 1 were waited for; matrix products, arithmetic and copies ran while one was open for 2% of the time, Pallas kernels for 11%

profile of v5, /device:TPU:0, one launch (start us, length us, event | category | flops | bytes accessed | tf_op | source)
XLA Modules:
  0.0 783.2 jit_solution(15325693182111884819)
XLA Ops:
  6.5 0.7 copy.309
  7.3 0.7 copy_convert_fusion
  8.1 0.7 maximum_bitcast_fusion
  8.8 3.2 slice_bitcast_fusion.6.x
  12.0 40.2 %attention.5 = (bf16[512,2048]{1,0:T(8,128)(2,1)}, bf16[512,2048]{1,0:T(8,128)(2,1)}) custom-call(bf16[512,2048]{1,0:T(8,128)(2,1)} %slice_bitcast_fusion.6.x, f32[1,2048]{1,0:T(1,128)} %bitcast.257, f32[1,2048]{1,0:T(1,128)} %bitcast.260, bf16[2048,2048]{1,0:T(8,128)(2,1)} %wq.1, bf16[2048,2048]{1,0:T(8,128)(2,1)} %wk.1, bf16[2048,2048]{1,0:T(8,128)(2,1)} %wv.1, ...), custom_call_target="tpu_custom_call" | custom-call | flops 200000000 | bytes 40000000 | tf_op jit(solution)/shard_map/attention/pallas_call | solution.py:73
  52.2 17.0 %all-gather.3.cloned.1.call-done = f32[64,16,512]{2,1,0:T(8,128)} async-done(((f32[2,16,512]{2,1,0:T(8,128)}), f32[64,16,512]{2,1,0:T(8,128)}) %all-gather.3.cloned.1.call-update) | async-done | bytes 2097168 | tf_op jit(solution)/shard_map/all_gather | solution.py:529
  69.2 5.2 compare_reduce_fusion.1
  74.4 2.3 dynamic-slice_bitcast_fusion
  76.7 3.3 fusion.60
  80.0 0.1 copy.345
  80.6 3.3 fusion.54
  83.9 0.1 copy.339
  84.1 0.6 add_reduce_fusion.3
  85.7 0.6 add_reduce_fusion.2
  87.0 0.6 add_reduce_fusion.1
  88.3 0.6 add_reduce_fusion
  89.6 681.6 %conditional.1 = (bf16[2,1,512,2048]{3,2,0,1:T(8,128)(2,1)}) conditional(s32[]{:T(128)} %convert_element_type.182, (s32[2,1,512,6]{2,1,3,0:T(1,128)S(1)}, s32[]{:T(128)}, bf16[512,2048]{1,0:T(8,128)(2,1)}, bf16[2,1,512,2048]{3,2,1,0:T(8,128)(2,1)}, f32[2048]{0:T(1024)}, /*index=5*/f32[2048]{0:T(1024)}, bf16[2048,2048]{1,0:T(8,128)(2,1)}, ...), branch_computations={%region_24.31_spmd, %region_31.38_spmd} | conditional | flops 314655520 | bytes 78545280 | solution.py:613
  97.3 0.7 fusion.41
  98.1 0.2 copy.274
  98.3 0.2 copy.275
  98.5 0.4 convolution_convert_fusion.11
  98.9 1.1 convert_reduce_fusion.3
  100.0 0.1 copy.284
  100.1 0.2 copy.287
  100.3 1.1 select_select_fusion.3
  101.4 0.7 copy.288.pos
  102.1 5.3 lists.3
  107.4 0.4 collective-permute-start.2
  107.8 3.4 collective-permute-start.3
  111.2 0.9 copy.289
  112.1 0.9 copy.290
  113.0 0.4 convolution_convert_fusion.8
  113.4 1.1 convert_reduce_fusion.2
  114.5 0.1 copy.299
  114.6 0.7 broadcast_select_fusion.2
  115.3 0.1 copy.302
  115.5 3.2 slice_bitcast_fusion.3
  118.6 1.1 select_select_fusion.2
  119.7 0.7 copy.307.lists
  120.4 1.1 copy.355
  121.5 0.6 pad_add_fusion.3.spot
  122.1 6.8 routes.3
  128.9 40.3 %attention.4 = (bf16[512,2048]{1,0:T(8,128)(2,1)}, bf16[512,2048]{1,0:T(8,128)(2,1)}) custom-call(bf16[512,2048]{1,0:T(8,128)(2,1)} %bitcast.248, f32[1,2048]{1,0:T(1,128)} %bitcast.259, f32[1,2048]{1,0:T(1,128)} %bitcast.262, bf16[2048,2048]{1,0:T(8,128)(2,1)} %get-tuple-element.115.wq, bf16[2048,2048]{1,0:T(8,128)(2,1)} %get-tuple-element.116.wk, ...), custom_call_target="tpu_custom_call" | custom-call | flops 200000000 | bytes 40000000 | tf_op jit(solution)/shard_map/cond/branch_1_fun/attention/pallas_call | solution.py:73
  169.2 1.3 fusion.29
  170.6 1.3 fusion.34
  171.9 0.8 pad_add_fusion.2.homes
  172.8 598.2 %layer.3 = (bf16[2,512,2048]{2,1,0:T(8,128)(2,1)}, bf16[8,288,2048]{2,1,0:T(8,128)(2,1)}, bf16[8,288,2048]{2,1,0:T(8,128)(2,1)}, bf16[8,208,2048]{2,1,0:T(8,128)...) custom-call(bf16[288,2048]{1,0:T(8,128)(2,1)} %collective-permute-do, ...), custom_call_target="tpu_custom_call" | custom-call | tf_op jit(solution)/shard_map/cond/branch_1_fun/layer/pallas_call | solution.py:583
  771.2 4.8 copy.359
  (45 shorter events, 1.1 us)
Async XLA Ops:
  6.5 62.7 %all-gather.3.cloned.1.call-start = ((), (), s32[]{:S(2)}) async-start(), calls=%async_computation | async-start | bytes 2162688 | tf_op jit(solution)/shard_map/all_gather | solution.py:529
  52.2 37.4 %copy-start.14 = (s32[2,1,512,6]{2,1,3,0:T(1,128)S(1)}, s32[2,1,512,6]{2,1,3,0:T(1,128)}, u32[]{:S(2)}) copy-start(s32[2,1,512,6]{2,1,3,0:T(1,128)} %param.15) | copy-start | bytes 73732
  98.3 2.0 copy-start.3
  98.5 2.9 copy-start.5
  98.9 3.2 copy-start.11
  100.0 2.1 copy-start.16
  107.4 65.3 %collective-permute-start.2 = (bf16[288,2048]{1,0:T(8,128)(2,1)}, bf16[288,2048]{1,0:T(8,128)(2,1)}, u32[]{:S(2)}, u32[]{:S(2)}) collective-permute-start(bf16[288,2048]{1,0:T(8,128)(2,1)} %get-tuple-element.107), channel_id=1, source_target_pairs={{0,4},{4,8},{8,12},{12,0},{1,5},{5,9},{9,13},{13,1},{2,6},{6,10},{... | collective-permute-start | bytes 3538952 | tf_op jit(solution)/shard_map/cond/branch_1_fun/ppermute | solution.py:565
  107.8 64.9 %collective-permute-start.3 = (bf16[288,2048]{1,0:T(8,128)(2,1)}, bf16[288,2048]{1,0:T(8,128)(2,1)}, u32[]{:S(2)}, u32[]{:S(2)}) collective-permute-start(bf16[288,2048]{1,0:T(8,128)(2,1)} %get-tuple-element.108), channel_id=1, source_target_pairs={{0,12},{4,0},{8,4},{12,8},{1,13},{5,1},{9,5},{13,9},{2,14},{6,2},{... | collective-permute-start | bytes 3538952 | tf_op jit(solution)/shard_map/cond/branch_1_fun/ppermute | solution.py:565
  112.1 7.6 copy-start.7
  113.0 6.7 copy-start.9
  113.0 7.4 copy-start.1
  113.4 8.1 %copy-start.12 = (s32[4,512]{0,1:T(8,128)}, s32[4,512]{0,1:T(8,128)S(1)}, u32[]{:S(2)}) copy-start(s32[4,512]{0,1:T(8,128)S(1)} %convolution_convert_fusion.8) | copy-start | bytes 24580 | tf_op jit(solution)/shard_map/cond
  114.5 7.0 copy-start.18
Sparse Core Ops, SparseCore 0:
  10.2 58.9 all-gather.2

commit v6 on v5

--- a/solution.py
+++ b/solution.py
@@ -63,16 +63,17 @@
             z[rows] = rms(r, gm[...])
 
 
-def attention(x, ga, gm, wq, wk, wv, wo):
-    t, d = x.shape
+def attention(x, m, t, ga, gm, wq, wk, wv, wo):
+    d = x.shape[1]
     step = 4 * HEAD
     whole = pl.BlockSpec((t, d), lambda i: (0, 0))
+    taken = pl.BlockSpec((t, d), lambda i: (m, 0))
     gain = pl.BlockSpec((1, d), lambda i: (0, 0))
     down = pl.BlockSpec((d, step), lambda i: (0, i))
     out = jax.ShapeDtypeStruct((t, d), BF16)
     return pl.pallas_call(
         attention_kernel, grid=(wq.shape[1] // step,), out_shape=[out, out],
-        in_specs=[whole, gain, gain, down, down, down, pl.BlockSpec((step, d), lambda i: (i, 0))],
+        in_specs=[taken, gain, gain, down, down, down, pl.BlockSpec((step, d), lambda i: (i, 0))],
         out_specs=[whole, whole], scratch_shapes=[pltpu.VMEM((t, d), BF16), pltpu.VMEM((t, d), F32)],
         compiler_params=pltpu.CompilerParams(vmem_limit_bytes=67043328), name="attention",
         cost_estimate=pl.CostEstimate(flops=200_000_000, bytes_accessed=40_000_000, transcendentals=0),
@@ -103,10 +104,10 @@
 
 
 def routes_kernel(top, el, gap, spot, pay, px, pb, gb, tri):
-    nm, ep, _, t = pay.shape
+    _, _, nm, _, t = pay.shape
     nb, _, window = px.shape
     steps = nb // nm
-    row, chip, core = spot[0], spot[1], spot[2]
+    row, chip, core, dp = spot[0], spot[1], spot[2], spot[3]
     tri[...] = jnp.where(lax.broadcasted_iota(I32, (t, t), 0) < lax.broadcasted_iota(I32, (t, t), 1), 1.0, 0.0).astype(BF16)
     per = 2 * el
     first = (row * 2 + chip) * per
@@ -121,8 +122,8 @@
             k = core + far_core - 2 * core * far_core
             y = chip + far_chip - 2 * chip * far_chip
             p = lax.rem(row - r + steps, steps) * 4 + y * 2 + k
-            chosen = pay[m, p, 0:top, :]
-            gate = pay[m, p, top:2 * top, :]
+            chosen = pay[dp, p, m, 0:top, :]
+            gate = pay[dp, p, m, top:2 * top, :]
             hit = jnp.zeros((per, t), F32)
             g = jnp.zeros((per, t), F32)
             in_a = jnp.zeros((1, t), F32)
@@ -524,22 +525,22 @@
         me = row * ncol + col
         chip, core = col // 2, col % 2
 
-        pay = jnp.concatenate([idx.astype(F32), gates, jnp.zeros((nm, ns, seq, 16 - 2 * top), F32)], -1)
-        pay = jnp.swapaxes(pay.reshape(nm, t, 16), 1, 2)
-        every = lax.all_gather(pay, tok_axes)
-        every = every.reshape((-1, ep) + every.shape[1:])
-
         def halves(idx_, first):
             half = layer // 2
             return [jnp.any(idx_ // half == 2 * first + c, -2) for c in range(2)]
 
+        flat = x.reshape(nm * t, d)
+        chosen = jnp.swapaxes(idx.reshape(nm, t, top), 1, 2)
+
         def width_needed(gap):
-            need = 0
-            for r in range(nrow):
-                a, b = halves(every[:, :, :, :top].astype(I32), r)
-                na, nb, both = (jnp.sum(v.astype(I32), -1) for v in (a & ~b, b & ~a, a & b))
-                need = jnp.maximum(need, jnp.max(jnp.maximum(na, gap) + both + jnp.maximum(nb, gap)))
-            return need
+            a, b = halves(chosen[:, None], jnp.arange(nrow, dtype=I32)[:, None, None])
+            na, nb, both = (jnp.sum(v.astype(I32), -1) for v in (a & ~b, b & ~a, a & b))
+            return jnp.max(jnp.maximum(na, gap) + both + jnp.maximum(nb, gap))
+
+        need = jnp.full((nm, 16 - 2 * top, t), width_needed(WIDTH - WINDOW), F32)
+        pay = jnp.concatenate([chosen.astype(F32), jnp.swapaxes(gates.reshape(nm, t, top), 1, 2), need], 1)
+        every = lax.all_gather(pay, tok_axes)
+        every = every.reshape((-1, ep) + every.shape[1:])
 
         def places_of(a, b, gap, width):
             only = [ranks(v) for v in (a & ~b, a & b, b & ~a)]
@@ -547,15 +548,12 @@
             mid = jnp.maximum(na, gap)
             return jnp.where(a & b, mid + only[1], jnp.where(a, only[0], jnp.where(b, width - 1 - only[2], NONE)))
 
-        mine = lax.dynamic_index_in_dim(jnp.swapaxes(every, 1, 2), lax.axis_index("dp"), 0, keepdims=False)
-
         def lists_of(m, width, window):
             steps = lax.rem(row + jnp.arange(nrow, dtype=I32), nrow)
-            own = jnp.broadcast_to(idx[m].reshape(t, top).T[None], (nrow, top, t))
+            own = jnp.broadcast_to(chosen[m][None], (nrow, top, t))
             return places_of(*halves(own, steps[:, None, None]), width - window, width)
 
-        def layers(width, window, z0, h0, x):
-            lists = [lists_of(m, width, window) for m in range(nm)]
+        def layers(width, window, z0, h0, x, lists):
             out = jax.ShapeDtypeStruct((width, d), BF16)
             rows0 = pl.pallas_call(
                 list_kernel, out_shape=[out] * nrow, in_specs=[VMEM, VMEM], out_specs=[VMEM] * nrow, name="lists",
@@ -563,8 +561,8 @@
                 cost_estimate=pl.CostEstimate(flops=50_000_000, bytes_accessed=7_000_000, transcendentals=0),
             )(lists[0], z0)
             came = [lax.ppermute(rows0[r], "row", [(i, (i + r) % nrow) for i in range(nrow)]) for r in STEPS[0][:2]]
-            x1, _ = lax.optimization_barrier((x[1], rows0[0]))
-            h1, z1 = attention(x1.reshape(t, d), gattn, gmoe, wq, wk, wv, wo)
+            x1, _ = lax.optimization_barrier((x, rows0[0]))
+            h1, z1 = attention(x1, 1, t, gattn, gmoe, wq, wk, wv, wo)
             homes = jnp.stack([jnp.pad(a.T, ((0, 0), (0, LANES - nrow))) for a in lists])
             nb = nm * nrow
             rows = el * cap
@@ -575,7 +573,7 @@
                 in_specs=[SMEM, VMEM], out_specs=[VMEM] * 3, scratch_shapes=[pltpu.VMEM((t, t), BF16)], name="routes",
                 compiler_params=pltpu.CompilerParams(vmem_limit_bytes=67043328),
                 cost_estimate=pl.CostEstimate(flops=50_000_000, bytes_accessed=2_000_000, transcendentals=0),
-            )(jnp.stack([row, chip, core]).astype(I32), mine)
+            )(jnp.stack([row, chip, core, lax.axis_index("dp")]).astype(I32), every)
             wide = jax.ShapeDtypeStruct((nb, width, d), BF16)
             part = jax.ShapeDtypeStruct((nb, window, d), F32)
             exact = jax.ShapeDtypeStruct((nb, width, d), F32)
@@ -608,9 +606,11 @@
             )(*came, rows0[0], rows0[STEPS[0][2]], z1, h0, h1, lists[1], homes, px, pb, gb, w1, w3, w2)
             return y.reshape(nm, ns, seq, d)
 
-        h0, z0 = attention(x[0].reshape(t, d), gattn, gmoe, wq, wk, wv, wo)
-        fits = width_needed(WIDTH - WINDOW) <= WIDTH
-        return lax.cond(fits, functools.partial(layers, WIDTH, WINDOW), functools.partial(layers, t, t), z0, h0, x)
+        h0, z0 = attention(flat, 0, t, gattn, gmoe, wq, wk, wv, wo)
+        fits = jnp.max(every[:, :, 0, 2 * top, 0]) <= WIDTH
+        short, full = ([lists_of(m, *shape) for m in range(nm)] for shape in ((WIDTH, WINDOW), (t, t)))
+        return lax.cond(fits, lambda z, h, x, a, b: layers(WIDTH, WINDOW, z, h, x, a),
+                        lambda z, h, x, a, b: layers(t, t, z, h, x, b), z0, h0, flat, short, full)
 
     tok_spec = P(None, tok_axes)
     exp_spec = P(ep_axes)

time: 790 us -> 771 us (0.976)
  other arithmetic: 21.5 us -> 8.23 us
where the time goes in v6:
time: 771 us; the launch traced here: 763 us
  Pallas kernels  691 us (90%)
  local copies, waits for them, and re-layouts  20.3 us (3%)
  between operations  15.1 us (2%)
  waiting for transfers between devices  14.5 us (2%)
  other arithmetic  8.23 us (1%)
    pallas_call x1, Pallas kernels, layers(): pl.pallas_call(functools.partial(layer_kernel, cap, nrow), out_shape=[jax...  598 us
    pallas_call x2, Pallas kernels, attention(): pl.pallas_call(attention_kernel, grid=(wq.shape[1] // step,), out_shape=[...  80.3 us
  transfers between devices with their start and end apart: 3, of which 1 were waited for; matrix products, arithmetic and copies ran while one was open for 2% of the time, Pallas kernels for 11%

profile of v6, /device:TPU:0, one launch (start us, length us, event | category | flops | bytes accessed | tf_op | source)
XLA Modules:
  0.0 762.9 jit_solution(5704792984081098257)
XLA Ops:
  6.5 0.8 and_select_fusion
  7.3 1.4 copy_bitcast_fusion.1
  8.7 0.8 copy.211
  9.6 0.2 convert_reduce_fusion.2
  9.8 0.6 add_reduce_fusion
  11.3 0.6 copy.120
  11.9 40.1 %attention.5 = (bf16[512,2048]{1,0:T(8,128)(2,1)}, bf16[512,2048]{1,0:T(8,128)(2,1)}) custom-call(bf16[1024,2048]{1,0:T(8,128)(2,1)} %bitcast.90, f32[1,2048]{1,0:T(1,128)} %bitcast.104, f32[1,2048]{1,0:T(1,128)} %bitcast.107, bf16[2048,2048]{1,0:T(8,128)(2,1)} %wq.1, bf16[2048,2048]{1,0:T(8,128)(2,1)} %wk.1, bf16[2048,2048]{1,0:T(8,128)(2,1)} %wv.1, ...), custom_call_target="tpu_custom_call" | custom-call | flops 200000000 | bytes 40000000 | tf_op jit(solution)/shard_map/attention/pallas_call | solution.py:74
  52.0 0.8 fusion.25
  53.1 0.2 convolution_convert_fusion.4
  53.5 0.2 convolution_convert_fusion.3
  53.6 0.6 not_and_fusion
  54.3 0.8 convolution_convert_fusion.1
  55.0 0.8 convolution_convert_fusion.2
  55.8 0.8 convolution_convert_fusion
  56.6 14.5 %all-gather.3.cloned.1.call-done = f32[64,16,512]{2,1,0:T(8,128)} async-done(((f32[2,16,512]{2,1,0:T(8,128)}), f32[64,16,512]{2,1,0:T(8,128)}) %all-gather.3.cloned.1.call-update) | async-done | bytes 2097168 | tf_op jit(solution)/shard_map/all_gather | solution.py:542
  71.1 1.5 slice_reduce_fusion
  73.1 677.7 %conditional.1 = (bf16[2,1,512,2048]{3,2,0,1:T(8,128)(2,1)}) conditional(s32[]{:T(128)} %convert_element_type.33, (s32[4,512]{1,0:T(4,128)S(1)}, pred[4,512]{1,0:T(4,128)(4,1)S(1)}, pred[4,512]{1,0:T(4,128)(4,1)S(1)}, pred[4,512]{1,0:T(4,128)(4,1)S(1)}, s32[]{:T(128)}, /*index=5*/pred[4,512]{1,0:T(4,128)(4,1)S(1)}, pred[4,512]{1,0:T(4,128)(4,1)S(1)}, ...), branch_computations={%region_13.14_spmd, %region_14.15_spmd} | conditional | flops 300167936 | bytes 67719192 | solution.py:612
  80.0 0.2 copy.145
  80.2 0.2 copy.146
  80.4 0.2 copy.143
  80.6 0.2 copy.144
  80.8 0.2 copy.147
  81.0 0.2 copy.148
  81.9 0.7 copy-done.1
  82.6 0.7 copy.115.pos
  83.3 5.3 lists.3
  88.6 0.4 collective-permute-start.2
  89.0 3.4 collective-permute-start.3
  92.4 0.8 reduce_sum.71
  93.2 0.8 copy.154
  94.1 0.9 copy.153
  94.9 0.9 copy.152
  95.8 0.9 copy.151
  96.7 0.9 copy.150
  97.5 0.9 copy.149
  98.4 0.8 copy.162
  99.2 0.8 copy.160
  100.1 0.8 copy.158
  100.9 0.2 fusion.4
  101.1 0.7 copy-done.3
  101.8 0.7 copy.116.lists
  102.5 0.6 pad_add_fusion.3.spot
  103.1 7.1 routes.3
  110.2 40.2 %attention.4 = (bf16[512,2048]{1,0:T(8,128)(2,1)}, bf16[512,2048]{1,0:T(8,128)(2,1)}) custom-call(bf16[1024,2048]{1,0:T(8,128)(2,1)} %get-tuple-element.234.x, f32[1,2048]{1,0:T(1,128)} %bitcast.106, f32[1,2048]{1,0:T(1,128)} %bitcast.109, bf16[2048,2048]{1,0:T(8,128)(2,1)} %get-tuple-element.237.wq, bf16[2048,2048]{1,0:T(8,128)(2,1)} %get-tuple-element.238.wk, ...), custom_call_target="tpu_custom_call" | custom-call | flops 200000000 | bytes 40000000 | tf_op jit(solution)/shard_map/cond/branch_1_fun/attention/pallas_call | solution.py:74
  150.4 1.1 pad_bitcast_fusion.2
  151.5 0.8 pad_add_fusion.2.homes
  152.3 598.3 %layer.3 = (bf16[2,512,2048]{2,1,0:T(8,128)(2,1)}, bf16[8,288,2048]{2,1,0:T(8,128)(2,1)}, bf16[8,288,2048]{2,1,0:T(8,128)(2,1)}, bf16[8,208,2048]{2,1,0:T(8,128)...) custom-call(bf16[288,2048]{1,0:T(8,128)(2,1)} %collective-permute-do, ...), custom_call_target="tpu_custom_call" | custom-call | tf_op jit(solution)/shard_map/cond/branch_1_fun/layer/pallas_call | solution.py:581
  750.9 4.8 copy.215
  (35 shorter events, 1.5 us)
Async XLA Ops:
  6.5 64.5 %all-gather.3.cloned.1.call-start = ((), (), s32[]{:S(2)}) async-start(), calls=%async_computation | async-start | bytes 2162688 | tf_op jit(solution)/shard_map/all_gather | solution.py:542
  53.1 2.8 copy-start.5
  53.1 2.8 copy-start.6
  54.3 0.8 copy-start.4
  54.3 1.6 copy-start.7
  54.3 1.6 copy-start.8
  81.9 0.7 copy-start.1
  88.6 63.7 %collective-permute-start.2 = (bf16[288,2048]{1,0:T(8,128)(2,1)}, bf16[288,2048]{1,0:T(8,128)(2,1)}, u32[]{:S(2)}, u32[]{:S(2)}) collective-permute-start(bf16[288,2048]{1,0:T(8,128)(2,1)} %get-tuple-element.229), channel_id=1, source_target_pairs={{0,4},{4,8},{8,12},{12,0},{1,5},{5,9},{9,13},{13,1},{2,6},{6,10},{... | collective-permute-start | bytes 3538952 | tf_op jit(solution)/shard_map/cond/branch_1_fun/ppermute | solution.py:563
  89.0 63.3 %collective-permute-start.3 = (bf16[288,2048]{1,0:T(8,128)(2,1)}, bf16[288,2048]{1,0:T(8,128)(2,1)}, u32[]{:S(2)}, u32[]{:S(2)}) collective-permute-start(bf16[288,2048]{1,0:T(8,128)(2,1)} %get-tuple-element.230), channel_id=1, source_target_pairs={{0,12},{4,0},{8,4},{12,8},{1,13},{5,1},{9,5},{13,9},{2,14},{6,2},{... | collective-permute-start | bytes 3538952 | tf_op jit(solution)/shard_map/cond/branch_1_fun/ppermute | solution.py:563
  101.1 0.7 copy-start.3
Sparse Core Ops, SparseCore 0:
  12.0 58.9 all-gather.2
